TPU v7x, 32 devices: a 4x4x1 block of a 4x4x8 slice. The times are simulated.
32 devices in a mesh: dp: 1 (over z), tp: 4 (over y), ep: 8 (over x, core).
Axes of the slice: x: 4, y: 4, z: 1, core: 2. Of those that a mesh axis runs over, the one named last changes fastest.
The devices are a block of a 4x4x8 slice.
Arguments:
- hidden: bfloat16 [256, 2048], P(('dp', 'ep'))
- seq_lens: int32 [256], P(('dp', 'ep'))
- rope_cos: float32 [256, 64], P(('dp', 'ep'))
- rope_sin: float32 [256, 64], P(('dp', 'ep'))
- ln1_scale: bfloat16 [2048], replicated
- ln1_bias: bfloat16 [2048], replicated
- w_qkv: bfloat16 [2048, 5120], P(None, 'tp')
- b_qkv: bfloat16 [5120], P('tp')
- w_out: bfloat16 [4096, 2048], P('tp')
- b_out: bfloat16 [2048], replicated
- k_cache: bfloat16 [256, 256, 4, 128], P(('dp', 'ep'), None, 'tp')
- v_cache: bfloat16 [256, 256, 4, 128], P(('dp', 'ep'), None, 'tp')
- ln2_scale: bfloat16 [2048], replicated
- ln2_bias: bfloat16 [2048], replicated
- w_router: bfloat16 [2048, 128], replicated
- expert_ids: int32 [256, 8], P(('dp', 'ep'))
- w_gate: bfloat16 [128, 2048, 768], P('ep', None, 'tp')
- w_up: bfloat16 [128, 2048, 768], P('ep', None, 'tp')
- w_down: bfloat16 [128, 768, 2048], P('ep', 'tp')
Outputs:
- output 1: bfloat16 [256, 2048], P(('dp', 'ep'))
- output 2: bfloat16 [256, 256, 4, 128], P(('dp', 'ep'), None, 'tp')
- output 3: bfloat16 [256, 256, 4, 128], P(('dp', 'ep'), None, 'tp')
All inputs are finite; a program needn't handle non-finite values.
Results may differ from a plain program's by a relative error of at most 0.0117888.
Values are sent between devices in bfloat16 or wider.
A program may use at most 768 MiB of HBM per device.

v0:
```python
import jax
import jax.numpy as jnp
from jax import lax
from jax.sharding import PartitionSpec as P

EPS = 1e-5


def layer_norm(values, ln_scale, ln_bias):
    vals_f32 = values.astype(jnp.float32)
    row_mean = jnp.mean(vals_f32, axis=-1, keepdims=True)
    centered = vals_f32 - row_mean
    row_var = jnp.mean(centered * centered, axis=-1, keepdims=True)
    normed = centered * lax.rsqrt(row_var + EPS)
    return (normed * ln_scale.astype(jnp.float32) + ln_bias.astype(jnp.float32)).astype(jnp.bfloat16)


def apply_rope(values, cos_part, sin_part):
    half_dim = values.shape[-1] // 2
    vals_f32 = values.astype(jnp.float32)
    first_half = vals_f32[..., :half_dim]
    second_half = vals_f32[..., half_dim:]
    rotated = jnp.concatenate([first_half * cos_part - second_half * sin_part, second_half * cos_part + first_half * sin_part], axis=-1)
    return rotated.astype(jnp.bfloat16)


def attention_part(normed, seq_lens, rope_cos, rope_sin, w_qkv, b_qkv, w_out, k_cache, v_cache):
    n_batch, s_max, n_groups, head_dim = k_cache.shape
    q_per = w_qkv.shape[1] // (n_groups * head_dim) - 2
    qkv_rows = (jnp.dot(normed, w_qkv, preferred_element_type=jnp.float32) + b_qkv.astype(jnp.float32)).astype(jnp.bfloat16)
    qkv_rows = qkv_rows.reshape(n_batch, n_groups, q_per + 2, head_dim)
    queries = apply_rope(qkv_rows[:, :, :q_per], rope_cos[:, None, None, :], rope_sin[:, None, None, :])
    key_new = apply_rope(qkv_rows[:, :, q_per], rope_cos[:, None, :], rope_sin[:, None, :])
    value_new = qkv_rows[:, :, q_per + 1]
    positions = jnp.arange(s_max)
    write_mask = (positions[None, :] == seq_lens[:, None])[:, :, None, None]
    k_cache_out = jnp.where(write_mask, key_new[:, None], k_cache)
    v_cache_out = jnp.where(write_mask, value_new[:, None], v_cache)
    scores = jnp.einsum('bgqh,bsgh->bgqs', queries, k_cache_out, preferred_element_type=jnp.float32) * head_dim ** -0.5
    in_range = positions[None, None, None, :] <= seq_lens[:, None, None, None]
    attn_probs = jax.nn.softmax(jnp.where(in_range, scores, -jnp.inf), axis=-1).astype(jnp.bfloat16)
    context = jnp.einsum('bgqs,bsgh->bgqh', attn_probs, v_cache_out, preferred_element_type=jnp.float32).astype(jnp.bfloat16)
    attn_part = jnp.dot(context.reshape(n_batch, n_groups * q_per * head_dim), w_out, preferred_element_type=jnp.float32)
    return attn_part, k_cache_out, v_cache_out


def route_tables(expert_ids, gate_probs, first_expert, n_exp, capacity):
    id_match = expert_ids[..., None] == (first_expert + jnp.arange(n_exp))
    chosen_mask = jnp.sum(id_match.astype(jnp.int32), axis=-2)
    slot_rank = jnp.cumsum(chosen_mask, axis=-2) - chosen_mask
    slot_of = jnp.swapaxes(jnp.where(chosen_mask > 0, slot_rank, -1), -1, -2)
    dispatch = (slot_of[..., None, :] == jnp.arange(capacity)[:, None]).astype(jnp.bfloat16)
    gate_dense = jnp.sum(jnp.where(id_match, gate_probs[..., None].astype(jnp.float32), 0.0), axis=-2)
    combine = dispatch * jnp.swapaxes(gate_dense, -1, -2)[..., None, :].astype(jnp.bfloat16)
    return dispatch, combine


def expert_ffn(routed_rows, w_gate, w_up, w_down):
    gate_pre = jnp.einsum('secd,edf->escf', routed_rows, w_gate, preferred_element_type=jnp.float32)
    up_pre = jnp.einsum('secd,edf->escf', routed_rows, w_up, preferred_element_type=jnp.float32)
    hidden_act = (jax.nn.silu(gate_pre) * up_pre).astype(jnp.bfloat16)
    return jnp.einsum('escf,efd->escd', hidden_act, w_down, preferred_element_type=jnp.float32)


def solution(mesh):
    n_ep = mesh.shape['ep']
    token_rows = P(('dp', 'ep'), None)
    token_vec = P(('dp', 'ep'))
    cache_spec = P(('dp', 'ep'), None, 'tp', None)
    expert_in = P('ep', None, 'tp')
    expert_down = P('ep', 'tp', None)

    def device_step(hidden, seq_lens, rope_cos, rope_sin, ln1_scale, ln1_bias, w_qkv, b_qkv, w_out, b_out, k_cache, v_cache, ln2_scale, ln2_bias, w_router, expert_ids, w_gate, w_up, w_down):
        n_batch, d_model = hidden.shape
        e_local = w_gate.shape[0]
        n_exp = e_local * n_ep
        top_k = expert_ids.shape[1]
        capacity = (2 * top_k * n_batch + n_exp - 1) // n_exp
        normed = layer_norm(hidden, ln1_scale, ln1_bias)
        attn_part, k_cache_out, v_cache_out = attention_part(normed, seq_lens, rope_cos, rope_sin, w_qkv, b_qkv, w_out, k_cache, v_cache)
        attn_sum = lax.psum(attn_part.astype(jnp.bfloat16), 'tp')
        hidden_mid = (hidden.astype(jnp.float32) + attn_sum.astype(jnp.float32) + b_out.astype(jnp.float32)).astype(jnp.bfloat16)
        normed2 = layer_norm(hidden_mid, ln2_scale, ln2_bias)
        logits = jnp.dot(normed2, w_router, preferred_element_type=jnp.float32)
        gate_probs = jax.nn.softmax(jnp.take_along_axis(logits, expert_ids, axis=1), axis=-1).astype(jnp.bfloat16)
        dispatch, combine = route_tables(expert_ids, gate_probs, 0, n_exp, capacity)
        outgoing = jnp.einsum('ecb,bd->ecd', dispatch, normed2, preferred_element_type=jnp.float32).astype(jnp.bfloat16)
        received = lax.all_to_all(outgoing, 'ep', 0, 0, tiled=True).reshape(n_ep, e_local, capacity, d_model)
        down_part = expert_ffn(received, w_gate, w_up, w_down).astype(jnp.bfloat16)
        expert_out = lax.psum(down_part, 'tp')
        returned = lax.all_to_all(expert_out, 'ep', 1, 0, tiled=True).reshape(n_exp, capacity, d_model)
        moe_sum = jnp.einsum('ecb,ecd->bd', combine, returned, preferred_element_type=jnp.float32)
        hidden_out = (hidden_mid.astype(jnp.float32) + moe_sum).astype(jnp.bfloat16)
        return hidden_out, k_cache_out, v_cache_out

    in_specs = (token_rows, token_vec, token_rows, token_rows, P(), P(), P(None, 'tp'), P('tp'), P('tp', None), P(), cache_spec, cache_spec, P(), P(), P(), token_rows, expert_in, expert_in, expert_down)
    return jax.shard_map(device_step, mesh=mesh, in_specs=in_specs, out_specs=(token_rows, cache_spec, cache_spec), check_vma=False)
```

profile of v0, /device:TPU:97, one launch (start us, length us, event | category | flops | bytes accessed | tf_op | source)
XLA Modules:
  0.0 226.1 jit_solution(31877109708449726)
XLA Ops:
  7.2 0.0 copy-start
  7.2 0.1 all-reduce.3.cloned.1.call-start
  7.3 1.1 convert_reduce_fusion.1
  8.3 1.1 fusion.48
  9.5 0.7 convert_element_type.115
  10.2 0.7 convert_element_type.116
  10.9 0.7 convert_element_type.118
  11.6 0.0 copy-start.3
  11.6 3.6 %fusion.12 = bf16[32,1280]{1,0:T(8,128)(2,1)S(1)} fusion(bf16[2048,1280]{1,0:T(8,128)(2,1)} %param.25, bf16[32,2048]{1,0:T(8,128)(2,1)} %param.19, f32[2048]{0:T(1024)S(1)} %convert_element_type.116, f32[2048]{0:T(1024)S(1)} %convert_element_type.115, f32[32]{0:T(128)S(1)} %add_rsqrt_fusion.1, f32[32]{0:T(128)S(1)} %broadcast_multiply_fusion.1, ...), kind=kOutput, calls=%fused_computation.14 | convolution fusion | flops 168247296 | bytes 5477632 | tf_op jit(solution)/shard_map/dot_general | solution.py:30
  15.2 0.1 reshape.223
  15.3 0.0 copy-done.9
  15.3 0.1 iota_compare_fusion.4
  15.4 0.0 copy-done.3
  15.4 0.0 copy-done.4
  15.4 0.1 fusion.81
  15.5 0.1 fusion.61
  15.7 0.1 pad_maximum_fusion
  15.7 4.8 %broadcast_select_fusion.1 = (bf16[32,256,1,128]{3,1,2,0:T(8,128)(2,1)S(1)}, bf16[32,256,1,128]{3,1,2,0:T(8,128)(2,1)}) fusion(bf16[32,256,1,128]{3,1,2,0:T(8,128)(2,1)} %param.29, pred[32,256]{1,0:T(8,128)(4,1)S(1)} %get-tuple-element.14, bf16[32,128]{1,0:T(8,128)(2,1)S(1)} %pad_maximum_fusion, bf16[32,256,1,128]{3,1,2,0:T(8,128)(2,1)} %param.30, ...), kind=kLoop, calls=%fused_computation.21 | loop fusion | flops 2097152 | bytes 8413184 | tf_op jit(solution)/shard_map/jit(_where)/select_n | solution.py:37
  20.5 0.7 fusion.33
  21.2 0.2 fusion.89
  21.4 2.2 fusion.37
  23.5 0.0 copy-done.1
  23.5 0.0 copy-start.5
  23.6 0.0 copy-start.6
  23.6 0.0 copy-start.7
  23.6 0.0 copy-start.8
  23.6 0.0 copy-start.2
  23.6 3.7 %convolution_convert_fusion.1 = bf16[32,2048]{1,0:T(8,128)(2,1)} fusion(bf16[1024,2048]{1,0:T(8,128)(2,1)} %param.27, bf16[4,8,8,128]{3,2,1,0:T(8,128)(2,1)S(1)} %bitcast.109), kind=kOutput, calls=%fused_computation.15 | convolution fusion | flops 134283264 | bytes 4390912 | tf_op jit(solution)/shard_map/dot_general | solution.py:43
  27.3 0.1 all-reduce.3.cloned.1.call-update
  27.4 0.1 all-reduce.5.cloned.1.call-start
  27.5 0.0 copy-done.5
  27.5 0.0 copy-done.6
  27.5 0.0 copy-done.7
  27.5 0.0 copy-done.8
  27.5 0.1 copy.48
  27.6 0.1 convert_reduce_fusion.2
  27.7 0.1 reduce_window_sum.11
  27.8 38.0 %all-reduce.3.cloned.1.call-done = bf16[32,2048]{1,0:T(8,128)(2,1)} async-done(((bf16[32,2048]{1,0:T(8,128)(2,1)}), bf16[32,2048]{1,0:T(8,128)(2,1)}) %all-reduce.3.cloned.1.call-update) | async-done | bytes 131088 | tf_op jit(solution)/shard_map/psum | solution.py:81
  65.7 0.0 copy-done.2
  65.7 1.1 convert_reduce_fusion
  66.8 0.2 fusion.44
  67.0 0.8 convolution_convert_fusion
  67.8 1.6 copy.52
  69.5 32.9 %all_to_all.20 = bf16[128,4,2048]{2,1,0:T(4,128)(2,1)S(1)} all-to-all(bf16[128,4,2048]{2,1,0:T(4,128)(2,1)S(1)} %copy.52), channel_id=1, replica_groups=mesh['dp'=1,'tp'=4,'ep'=8] {'ep'}, dimensions={0} | all-to-all | bytes 4194304 | tf_op jit(solution)/shard_map/all_to_all | solution.py:88
  102.4 1.2 copy.53
  103.5 8.5 %fusion.5 = f32[16,8,4,192]{3,1,2,0:T(8,128)S(1)} fusion(bf16[16,2048,192]{1,2,0:T(8,128)(2,1)} %param.35, bf16[8,16,4,2048]{3,1,0,2:T(8,128)(2,1)S(1)} %bitcast.106), kind=kOutput, calls=%fused_computation.6 | convolution fusion | flops 402653184 | bytes 15073280 | tf_op jit(solution)/shard_map/secd,edf->escf/dot_general | solution.py:59
  112.0 8.5 %fusion.25 = bf16[16,8,4,192]{3,1,2,0:T(8,128)(2,1)S(1)} fusion(bf16[16,2048,192]{1,2,0:T(8,128)(2,1)} %param.36, bf16[8,16,4,2048]{3,1,0,2:T(8,128)(2,1)S(1)} %bitcast.107, f32[16,8,4,192]{3,1,2,0:T(8,128)S(1)} %fusion.5), kind=kOutput, calls=%fused_computation.26 | convolution fusion | flops 403243008 | bytes 15269888 | tf_op jit(solution)/shard_map/secd,edf->escf/dot_general | solution.py:60
  120.6 8.2 %fusion.7 = bf16[16,8,4,2048]{3,1,2,0:T(8,128)(2,1)} fusion(bf16[16,8,4,192]{3,1,2,0:T(8,128)(2,1)S(1)} %fusion.25, bf16[16,192,2048]{2,1,0:T(8,128)(2,1)} %param.37), kind=kOutput, calls=%fused_computation.8 | convolution fusion | flops 403701760 | bytes 14876672 | tf_op jit(solution)/shard_map/escf,efd->escd/dot_general | solution.py:62
  128.8 0.1 all-reduce.5.cloned.1.call-update
  128.8 52.4 %all-reduce.5.cloned.1.call-done = bf16[16,8,4,2048]{3,1,2,0:T(8,128)(2,1)} async-done(((bf16[16,8,4,2048]{3,1,2,0:T(8,128)(2,1)}), bf16[16,8,4,2048]{3,1,2,0:T(8,128)(2,1)}) %all-reduce.5.cloned.1.call-update) | async-done | bytes 2097168 | tf_op jit(solution)/shard_map/psum | solution.py:90
  181.2 4.5 %copy.56 = bf16[16,8,4,2048]{3,2,0,1:T(4,128)(2,1)} copy(bf16[16,8,4,2048]{3,1,2,0:T(8,128)(2,1)} %all-reduce.5.cloned.1.call-done) | data formatting | bytes 4194304 | tf_op jit(solution)/shard_map/psum | solution.py:90
  185.7 5.2 %all-to-all-start.1 = ((bf16[16,8,4,2048]{3,2,0,1:T(4,128)(2,1)}), bf16[16,8,4,2048]{3,2,0,1:T(4,128)(2,1)S(1)}, u32[]{:S(2)}, u32[]{:S(2)}) async-start(bf16[16,8,4,2048]{3,2,0,1:T(4,128)(2,1)} %copy.56), calls=%async_computation.1 | async-start | bytes 4194304 | tf_op jit(solution)/shard_map/all_to_all | solution.py:91
  190.9 0.1 reshape.231
  191.0 0.0 copy-done
  191.0 0.3 fusion.86
  191.3 1.9 gather_fusion
  193.2 0.1 reshape.234
  193.3 0.1 fusion.84
  193.4 0.2 fusion.78
  193.6 0.1 fusion.79
  193.7 0.2 select_reduce_fusion
  193.9 23.1 %all-to-all-done.1 = bf16[16,8,4,2048]{3,2,0,1:T(4,128)(2,1)S(1)} async-done(((bf16[16,8,4,2048]{3,2,0,1:T(4,128)(2,1)}), bf16[16,8,4,2048]{3,2,0,1:T(4,128)(2,1)S(1)}, u32[]{:S(2)}, u32[]{:S(2)}) %all-to-all-start.1) | async-done | bytes 2097184 | tf_op jit(solution)/shard_map/all_to_all | solution.py:91
  216.9 1.2 copy.57
  218.1 1.1 fusion.11
  (15 shorter events, 0.1 us)
Async XLA Ops:
  7.2 183.9 %copy-start = (bf16[2048,128]{1,0:T(8,128)(2,1)S(1)}, bf16[2048,128]{1,0:T(8,128)(2,1)}, u32[]{:S(2)}) copy-start(bf16[2048,128]{1,0:T(8,128)(2,1)} %param.33) | copy-start | bytes 1572868
  7.2 58.6 %all-reduce.3.cloned.1.call-start = ((), (), s32[]{:S(2)}) async-start(), calls=%async_computation.2 | async-start | bytes 262144 | tf_op jit(solution)/shard_map/psum | solution.py:81
  11.5 3.8 %copy-start.9 = (s32[32]{0:T(128)S(1)}, s32[32]{0:T(128)}, u32[]{:S(2)}) copy-start(s32[32]{0:T(128)} %param.20) | copy-start | bytes 388
  11.6 3.9 %copy-start.3 = (f32[32,64]{1,0:T(8,128)S(1)}, f32[32,64]{1,0:T(8,128)}, u32[]{:S(2)}) copy-start(f32[32,64]{1,0:T(8,128)} %param.22) | copy-start | bytes 24580
  11.6 3.9 %copy-start.4 = (f32[32,64]{1,0:T(8,128)S(1)}, f32[32,64]{1,0:T(8,128)}, u32[]{:S(2)}) copy-start(f32[32,64]{1,0:T(8,128)} %param.21) | copy-start | bytes 24580
  20.5 3.1 %copy-start.1 = (bf16[32,256,1,128]{3,1,2,0:T(8,128)(2,1)}, bf16[32,256,1,128]{3,1,2,0:T(8,128)(2,1)S(1)}, u32[]{:S(2)}) copy-start(bf16[32,256,1,128]{3,1,2,0:T(8,128)(2,1)S(1)} %get-tuple-element.11) | copy-start | bytes 6291460
  23.5 3.9 %copy-start.5 = (bf16[2048]{0:T(1024)(128)(2,1)S(1)}, bf16[2048]{0:T(1024)(128)(2,1)}, u32[]{:S(2)}) copy-start(bf16[2048]{0:T(1024)(128)(2,1)} %param.31) | copy-start | bytes 12292
  23.6 3.9 %copy-start.6 = (bf16[2048]{0:T(1024)(128)(2,1)S(1)}, bf16[2048]{0:T(1024)(128)(2,1)}, u32[]{:S(2)}) copy-start(bf16[2048]{0:T(1024)(128)(2,1)} %param.32) | copy-start | bytes 12292
  23.6 3.9 %copy-start.7 = (bf16[2048]{0:T(1024)(128)(2,1)S(1)}, bf16[2048]{0:T(1024)(128)(2,1)}, u32[]{:S(2)}) copy-start(bf16[2048]{0:T(1024)(128)(2,1)} %param.28) | copy-start | bytes 12292
  23.6 3.9 %copy-start.8 = (s32[32,8]{0,1:T(8,128)S(1)}, s32[32,8]{0,1:T(8,128)}, u32[]{:S(2)}) copy-start(s32[32,8]{0,1:T(8,128)} %param.34) | copy-start | bytes 3076
  23.6 42.2 %copy-start.2 = (bf16[32,2048]{1,0:T(8,128)(2,1)S(1)}, bf16[32,2048]{1,0:T(8,128)(2,1)}, u32[]{:S(2)}) copy-start(bf16[32,2048]{1,0:T(8,128)(2,1)} %param.19) | copy-start | bytes 393220
  27.4 153.9 %all-reduce.5.cloned.1.call-start = ((), (), s32[]{:S(2)}) async-start(), calls=%async_computation.3 | async-start | bytes 4194304 | tf_op jit(solution)/shard_map/psum | solution.py:90
  185.7 31.2 %all-to-all-start.1 = ((bf16[16,8,4,2048]{3,2,0,1:T(4,128)(2,1)}), bf16[16,8,4,2048]{3,2,0,1:T(4,128)(2,1)S(1)}, u32[]{:S(2)}, u32[]{:S(2)}) async-start(bf16[16,8,4,2048]{3,2,0,1:T(4,128)(2,1)} %copy.56), calls=%async_computation.1 | async-start | bytes 4194304 | tf_op jit(solution)/shard_map/all_to_all | solution.py:91
Sparse Core Ops, SparseCore 0:
  27.5 38.1 all-reduce.2
  128.9 52.2 all-reduce.4
where the time goes:
time: 227 us; the launch traced here: 226 us
  waiting for transfers between devices  114 us (50%)
  matrix products  37.6 us (17%)
  blocking collectives  32.9 us (14%)
  between operations  14.3 us (6%)
  other arithmetic  11.7 us (5%)
  local copies, waits for them, and re-layouts  10.7 us (5%)
  starting transfers between devices  5.32 us (2%)
    psum x1, waiting for transfers between devices, device_step(): expert_out = lax.psum(down_part, 'tp')  52.4 us
    psum x1, waiting for transfers between devices, device_step(): attn_sum = lax.psum(attn_part.astype(jnp.bfloat16), 'tp')  38 us
    all_to_all x1, blocking collectives, device_step(): lax.all_to_all(outgoing, 'ep', 0, 0, tiled=True)  32.9 us
    all_to_all x1, waiting for transfers between devices, device_step(): lax.all_to_all(expert_out, 'ep', 1, 0, tiled=True)  23.1 us
    dot_general x1, matrix products, expert_ffn(): jnp.einsum('secd,edf->escf', routed_rows, w_up, preferred_element_type=jn...  8.51 us
    dot_general x1, matrix products, expert_ffn(): jnp.einsum('secd,edf->escf', routed_rows, w_gate, preferred_element_type=...  8.49 us
    dot_general x1, matrix products, expert_ffn(): jnp.einsum('escf,efd->escd', hidden_act, w_down, preferred_element_type=j...  8.21 us
    all_to_all x1, starting transfers between devices, device_step(): lax.all_to_all(expert_out, 'ep', 1, 0, tiled=True)  5.19 us
  transfers between devices with their start and end apart: 3, of which 3 were waited for; matrix products, arithmetic and copies ran while one was open for 1% of the time, Pallas kernels for 0%

commit v1 on v0

v1 whole, which is shorter than its diff:
```python
import functools

import jax
import jax.numpy as jnp
from jax import lax
from jax.experimental import pallas as pl
from jax.experimental.pallas import tpu as pltpu
from jax.sharding import PartitionSpec as P

EPS = 1e-5
F32 = jnp.float32
BF16 = jnp.bfloat16
MESH = pl.DeviceIdType.MESH
NT = (((1,), (1,)), ((), ()))


def row_norm(vals_f32, ln_scale, ln_bias):
    row_mean = jnp.mean(vals_f32, axis=-1, keepdims=True)
    centered = vals_f32 - row_mean
    row_var = jnp.mean(centered * centered, axis=-1, keepdims=True)
    normed = centered * lax.rsqrt(row_var + EPS)
    return (normed * ln_scale + ln_bias).astype(BF16)


def row_of(ref):
    return ref[...].astype(F32)[None, :]


def attention_kernel(n_qkv, group, seq_ref, hid_ref, cos_ref, sin_ref, lns_ref, lnb_ref, bqkv_ref, wqkv_hbm, k_hbm, v_hbm, wout_hbm,
                     part_ref, kout_hbm, vout_hbm,
                     wqkv, kbuf, vbuf, wout, q_s, c_s, new_s, ctx, sem_w, sem_k, sem_v, sem_o, sem_ko, sem_vo):
    n_batch, s_max, head = kbuf.shape
    n_q = q_s.shape[1]
    d_model = wqkv.shape[0]
    n_groups = n_batch // group
    step = d_model // n_qkv
    for i in range(n_qkv):
        rows = pl.ds(i * step, step)
        pltpu.make_async_copy(wqkv_hbm.at[rows], wqkv.at[rows], sem_w.at[i]).start()
    for g in range(n_groups):
        rows = pl.ds(g * group, group)
        pltpu.make_async_copy(k_hbm.at[rows], kbuf.at[rows], sem_k.at[g]).start()
        pltpu.make_async_copy(v_hbm.at[rows], vbuf.at[rows], sem_v.at[g]).start()
    pltpu.make_async_copy(wout_hbm, wout, sem_o.at[0]).start()

    normed = row_norm(hid_ref[...].astype(F32), row_of(lns_ref), row_of(lnb_ref))
    acc = jnp.broadcast_to(row_of(bqkv_ref), (n_batch, wqkv.shape[1]))
    total = None
    for i in range(n_qkv):
        rows = pl.ds(i * step, step)
        pltpu.make_async_copy(wqkv_hbm.at[rows], wqkv.at[rows], sem_w.at[i]).wait()
        one = jnp.dot(normed[:, i * step:(i + 1) * step], wqkv[rows, :], preferred_element_type=F32)
        total = one if total is None else total + one
    qkv = (total + acc).astype(BF16).astype(F32)
    cos = jnp.concatenate([cos_ref[...], cos_ref[...]], axis=-1)
    sin = jnp.concatenate([-sin_ref[...], sin_ref[...]], axis=-1)
    for j in range(n_q + 1):
        x = qkv[:, j * head:(j + 1) * head]
        rot = x * cos + pltpu.roll(x, head // 2, 1) * sin
        if j < n_q:
            q_s[:, j, :] = rot
        else:
            new_s[0] = rot
    new_s[1] = qkv[:, (n_q + 1) * head:]

    row_iota = lax.broadcasted_iota(jnp.int32, (16, head), 0)
    lane_iota = lax.broadcasted_iota(jnp.int32, (n_q, s_max), 1)

    def one_group(g, carry):
        rows = pl.ds(g * group, group)
        pltpu.make_async_copy(k_hbm.at[rows], kbuf.at[rows], sem_k.at[g]).wait()
        pltpu.make_async_copy(v_hbm.at[rows], vbuf.at[rows], sem_v.at[g]).wait()
        scores = []
        for i in range(group):
            b = g * group + i
            p = seq_ref[b]
            base = pl.multiple_of((p // 16) * 16, 16)
            hit = row_iota == (p - base)
            for buf, which in ((kbuf, 0), (vbuf, 1)):
                old = buf[b, pl.ds(base, 16), :].astype(F32)
                row = new_s[which, pl.ds(b, 1), :]
                buf[b, pl.ds(base, 16), :] = jnp.where(hit, row, old).astype(BF16)
        pltpu.make_async_copy(kbuf.at[rows], kout_hbm.at[rows], sem_ko.at[g]).start()
        pltpu.make_async_copy(vbuf.at[rows], vout_hbm.at[rows], sem_vo.at[g]).start()
        for i in range(group):
            b = g * group + i
            s = lax.dot_general(q_s[b].astype(BF16), kbuf[b], NT, preferred_element_type=F32) * head ** -0.5
            scores.append(jnp.where(lane_iota <= seq_ref[b], s, -jnp.inf))
        s = jnp.concatenate(scores, axis=0)
        e = jnp.exp(s - jnp.max(s, axis=-1, keepdims=True))
        probs = (e / jnp.sum(e, axis=-1, keepdims=True))
        for i in range(group):
            b = g * group + i
            c_s[b] = jnp.dot(probs[i * n_q:(i + 1) * n_q].astype(BF16), vbuf[b], preferred_element_type=F32)
        return carry

    lax.fori_loop(0, n_groups, one_group, 0)
    for j in range(n_q):
        ctx[:, j * head:(j + 1) * head] = c_s[:, j, :].astype(BF16)
    pltpu.make_async_copy(wout_hbm, wout, sem_o.at[0]).wait()
    part = jnp.dot(ctx[...], wout[...], preferred_element_type=F32)
    part_ref[...] = part.reshape(part_ref.shape).astype(BF16)
    for g in range(n_groups):
        rows = pl.ds(g * group, group)
        pltpu.make_async_copy(kbuf.at[rows], kout_hbm.at[rows], sem_ko.at[g]).wait()
        pltpu.make_async_copy(vbuf.at[rows], vout_hbm.at[rows], sem_vo.at[g]).wait()


def moe_kernel(n_tp, n_x, n_cols, part_hbm, hid_hbm, ids_hbm, bout_hbm, lns_hbm, lnb_hbm, wr_hbm, wg_hbm, wu_hbm, wd_hbm,
               out_hbm,
               part, hid, ids, bout, lns, lnb, wr, wg, wu, wd, mask_s, a_recv, x1_s, ga, gb, h_t, g_t, act,
               o32, c0_send, c0_recv, c1_send, c1_own, c1_recv, c2_send, c2_own, c2_recv, outbuf,
               sem_in, sem_w, a_ss, a_rs, b1_ss, b1_rs, b2_ss, b2_rs, b3_ss, b3_rs,
               c0_ss, c0_rs, c1_ss, c1_rs, c2_ss, c2_rs, d_ss, d_rs, sem_out):
    t = lax.axis_index('tp')
    e = lax.axis_index('ep')
    x = e // 2
    c = e % 2
    n_exp, ff, d_model = wg.shape
    half = d_model // 2
    d_col = d_model // n_cols

    def y_peer(dt):
        return {'tp': lax.rem(t + dt, n_tp)}

    def y_src(dt):
        return lax.rem(t + n_tp - dt, n_tp)

    def x_dst(dx):
        return lax.rem(x + dx, n_x)

    def x_peer(dx):
        return {'ep': 2 * x_dst(dx) + c}

    def x_src(dx):
        return lax.rem(x + n_x - dx, n_x)

    partner = {'ep': 2 * x + 1 - c}

    def rcopy(src, dst, ss, rs, dev):
        return pltpu.make_async_remote_copy(src_ref=src, dst_ref=dst, send_sem=ss, recv_sem=rs, device_id=dev, device_id_type=MESH)

    small = [(part_hbm, part), (hid_hbm, hid), (ids_hbm, ids), (bout_hbm, bout), (lns_hbm, lns), (lnb_hbm, lnb), (wr_hbm, wr)]
    copies = [pltpu.make_async_copy(s, d, sem_in.at[i]) for i, (s, d) in enumerate(small)]
    for cp in copies:
        cp.start()
    n_pair = n_exp // 2

    def wcopy(w, p):
        src, dst = ((wg_hbm, wg), (wu_hbm, wu), (wd_hbm, wd))[w]
        rows = pl.ds(2 * p, 2)
        return pltpu.make_async_copy(src.at[rows], dst.at[rows], sem_w.at[w, p])

    for p in range(n_pair):
        wcopy(0, p).start()
        wcopy(1, p).start()
    for p in range(n_pair):
        wcopy(2, p).start()

    barrier = pltpu.get_barrier_semaphore()
    for dt in range(1, n_tp):
        pl.semaphore_signal(barrier, inc=1, device_id=y_peer(dt), device_id_type=MESH)
    for dx in range(1, n_x):
        pl.semaphore_signal(barrier, inc=1, device_id=x_peer(dx), device_id_type=MESH)
    pl.semaphore_signal(barrier, inc=1, device_id=partner, device_id_type=MESH)
    for cp in copies:
        cp.wait()
    pl.semaphore_wait(barrier, n_tp + n_x - 1)

    a_send = []
    for dt in range(1, n_tp):
        cp = rcopy(part.at[lax.rem(t + dt, n_tp)], a_recv.at[dt - 1], a_ss.at[dt - 1], a_rs.at[dt - 1], y_peer(dt))
        cp.start()
        a_send.append(cp)

    n_all = wr.shape[1]
    exp_iota = lax.broadcasted_iota(jnp.int32, (n_all, ids.shape[1]), 0)
    picked = jnp.zeros((n_all, ids.shape[1]), F32)
    for k in range(ids.shape[0]):
        picked = picked + jnp.where(exp_iota == ids[k:k + 1, :], 1.0, 0.0)
    mask_s[...] = picked.T.reshape(mask_s.shape)
    base = part[t].astype(F32)
    for dt in range(1, n_tp):
        a_send[dt - 1].wait_recv()
    for dt in range(1, n_tp):
        base = base + a_recv[dt - 1].astype(F32)
    x1 = (hid[t].astype(F32) + base + row_of(bout)).astype(BF16)
    x1_s[...] = x1
    h2 = row_norm(x1.astype(F32), row_of(lns), row_of(lnb))

    ga[x, c, t] = h2[:, :half]
    b_send = []

    def send(src, dst, ss, rs, dev):
        cp = rcopy(src, dst, ss, rs, dev)
        cp.start()
        b_send.append(cp)
        return cp

    a1 = [send(ga.at[x, c, t], ga.at[x, c, t], b1_ss.at[0, dt - 1], b1_rs.at[0, dt - 1], y_peer(dt)) for dt in range(1, n_tp)]
    logits = jnp.dot(h2, wr[...], preferred_element_type=F32)
    keep = mask_s[t] > 0.5
    logits = jnp.where(keep, logits, -jnp.inf)
    ex = jnp.exp(logits - jnp.max(logits, axis=-1, keepdims=True))
    gates = (ex / jnp.sum(ex, axis=-1, keepdims=True)).astype(BF16)
    gb[x, c, t, :, 0:half] = h2[:, half:]
    gb[x, c, t, :, half:half + n_all] = gates
    b1 = [send(gb.at[x, c, t], gb.at[x, c, t], b1_ss.at[1, dx - 1], b1_rs.at[1, dx - 1], x_peer(dx)) for dx in range(1, n_x)]
    for cp in a1:
        cp.wait_recv()
    a2 = [send(ga.at[x, c], ga.at[x, c], b2_ss.at[0, dx - 1], b2_rs.at[0, dx - 1], x_peer(dx)) for dx in range(1, n_x)]
    a3 = [send(ga.at[x, c], ga.at[x, c], b3_ss.at[0, 0], b3_rs.at[0, 0], partner)]
    for cp in b1:
        cp.wait_recv()
    b2 = [send(gb.at[:, c, t], gb.at[:, c, t], b2_ss.at[1, dt - 1], b2_rs.at[1, dt - 1], y_peer(dt)) for dt in range(1, n_tp)]
    b3 = [send(gb.at[:, c, t], gb.at[:, c, t], b3_ss.at[1, 0], b3_rs.at[1, 0], partner)]
    for dx in range(1, n_x):
        a2[dx - 1].wait_recv()
        xs = x_src(dx)
        a3.append(send(ga.at[xs, c], ga.at[xs, c], b3_ss.at[0, dx], b3_rs.at[0, dx], partner))
    for dt in range(1, n_tp):
        b2[dt - 1].wait_recv()
        ts = y_src(dt)
        b3.append(send(gb.at[:, c, ts], gb.at[:, c, ts], b3_ss.at[1, dt], b3_rs.at[1, dt], partner))
    for cp in a3:
        cp.wait_recv()
    n_tok = n_x * 2 * n_tp * x1.shape[0]
    for k in range(half // 256):
        piece = ga[:, :, :, :, k * 256:(k + 1) * 256].astype(F32).reshape(n_tok, 256)
        h_t[pl.ds(k * 256, 256), :] = piece.T.astype(BF16)
    for cp in b3:
        cp.wait_recv()
    for k in range(half // 256):
        piece = gb[:, :, :, :, k * 256:(k + 1) * 256].astype(F32).reshape(n_tok, 256)
        h_t[pl.ds(half + k * 256, 256), :] = piece.T.astype(BF16)
    g_t[...] = gb[:, :, :, :, half:half + n_all].astype(F32).reshape(n_tok, n_all).T

    def one_pair(p, carry):
        wcopy(0, p).wait()
        wcopy(1, p).wait()
        rows = pl.ds(2 * p, 2)
        gate_pre = jnp.dot(wg[rows].reshape(2 * ff, d_model), h_t[...], preferred_element_type=F32)
        up_pre = jnp.dot(wu[rows].reshape(2 * ff, d_model), h_t[...], preferred_element_type=F32)
        a = (gate_pre * jax.nn.sigmoid(gate_pre) * up_pre).astype(BF16).astype(F32)
        g0 = g_t[pl.ds(e * n_exp + 2 * p, 1), :]
        g1 = g_t[pl.ds(e * n_exp + 2 * p + 1, 1), :]
        a = jnp.concatenate([a[:ff] * g0, a[ff:] * g1], axis=0)
        act[p] = a.T.astype(BF16)
        return carry

    lax.fori_loop(0, n_pair, one_pair, 0)
    for p in range(n_pair):
        wcopy(2, p).wait()

    c_send = []

    def csend(src, dst, ss, rs, dev):
        cp = rcopy(src, dst, ss, rs, dev)
        cp.start()
        c_send.append(cp)
        return cp

    c0, c1, c2, dd = {}, {}, {}, {}

    def down(j):
        cols = slice(j * d_col, (j + 1) * d_col)
        o = None
        for p in range(n_pair):
            one = jnp.dot(act[p], wd[2 * p:2 * p + 2, :, cols].reshape(2 * ff, d_col), preferred_element_type=F32)
            o = one if o is None else o + one
        o = o.reshape(n_x, 2, n_tp, n_tok // (2 * n_x * n_tp), d_col)
        o32[j] = o
        c0_send[j] = o.astype(BF16)
        c0[j] = csend(c0_send.at[j, :, 1 - c], c0_recv.at[j], c0_ss.at[j], c0_rs.at[j], partner)

    def stage1(j):
        c0[j].wait_recv()
        s = o32[j, :, c] + c0_recv[j].astype(F32)
        c1_send[j] = s.astype(BF16)
        c1_own[j] = s
        if j < n_cols // 2:
            c1[j] = [csend(c1_send.at[j, x_dst(dx)], c1_recv.at[j, dx - 1], c1_ss.at[j, dx - 1], c1_rs.at[j, dx - 1], x_peer(dx)) for dx in range(1, n_x)]
        else:
            c1[j] = [csend(c1_send.at[j, :, lax.rem(t + dt, n_tp)], c1_recv.at[j, dt - 1], c1_ss.at[j, dt - 1], c1_rs.at[j, dt - 1], y_peer(dt)) for dt in range(1, n_tp)]

    def stage2(j):
        for cp in c1[j]:
            cp.wait_recv()
        s = c1_own[j, x] if j < n_cols // 2 else c1_own[j, :, t]
        for i in range(len(c1[j])):
            s = s + c1_recv[j, i].astype(F32)
        c2_send[j] = s.astype(BF16)
        c2_own[j] = s
        if j < n_cols // 2:
            c2[j] = [csend(c2_send.at[j, lax.rem(t + dt, n_tp)], c2_recv.at[j, dt - 1], c2_ss.at[j, dt - 1], c2_rs.at[j, dt - 1], y_peer(dt)) for dt in range(1, n_tp)]
        else:
            c2[j] = [csend(c2_send.at[j, x_dst(dx)], c2_recv.at[j, dx - 1], c2_ss.at[j, dx - 1], c2_rs.at[j, dx - 1], x_peer(dx)) for dx in range(1, n_x)]

    def stage3(j):
        for cp in c2[j]:
            cp.wait_recv()
        s = c2_own[j, t] if j < n_cols // 2 else c2_own[j, x]
        for i in range(len(c2[j])):
            s = s + c2_recv[j, i].astype(F32)
        cols = slice(j * d_col, (j + 1) * d_col)
        outbuf[j, t] = (x1_s[:, cols].astype(F32) + s).astype(BF16)
        dd[j] = [csend(outbuf.at[j, t], outbuf.at[j, t], d_ss.at[j, dt - 1], d_rs.at[j, dt - 1], y_peer(dt)) for dt in range(1, n_tp)]

    for j in range(n_cols + 3):
        if j < n_cols:
            down(j)
        if 0 <= j - 1 < n_cols:
            stage1(j - 1)
        if 0 <= j - 2 < n_cols:
            stage2(j - 2)
        if 0 <= j - 3 < n_cols:
            stage3(j - 3)
    outs = []
    for j in range(n_cols):
        for cp in dd[j]:
            cp.wait_recv()
        cp = pltpu.make_async_copy(outbuf.at[j], out_hbm.at[:, :, pl.ds(j * d_col, d_col)], sem_out.at[j])
        cp.start()
        outs.append(cp)
    for cp in a_send + b_send + c_send:
        cp.wait_send()
    for cp in outs:
        cp.wait()


def solution(mesh):
    n_ep = mesh.shape['ep']
    n_tp = mesh.shape['tp']
    n_x = n_ep // 2
    token_rows = P(('dp', 'ep'), None)
    token_vec = P(('dp', 'ep'))
    cache_spec = P(('dp', 'ep'), None, 'tp', None)
    expert_in = P('ep', None, 'tp')
    expert_down = P('ep', 'tp', None)
    any_spec = pl.BlockSpec(memory_space=pl.ANY)
    vmem = pl.BlockSpec(memory_space=pltpu.VMEM)
    smem = pl.BlockSpec(memory_space=pltpu.SMEM)

    def device_step(hidden, seq_lens, rope_cos, rope_sin, ln1_scale, ln1_bias, w_qkv, b_qkv, w_out, b_out, k_cache, v_cache, ln2_scale, ln2_bias, w_router, expert_ids, w_gate, w_up, w_down):
        n_batch, d_model = hidden.shape
        _, s_max, n_kv, head = k_cache.shape
        n_q = w_qkv.shape[1] // head - 2
        rows = n_batch // n_tp
        n_qkv, group = 4, 8
        k3 = k_cache.reshape(n_batch, s_max, head)
        v3 = v_cache.reshape(n_batch, s_max, head)
        dma = pltpu.SemaphoreType.DMA
        part, k_out, v_out = pl.pallas_call(
            functools.partial(attention_kernel, n_qkv, group),
            out_shape=(jax.ShapeDtypeStruct((n_tp, rows, d_model), BF16), jax.ShapeDtypeStruct(k3.shape, BF16), jax.ShapeDtypeStruct(v3.shape, BF16)),
            in_specs=[smem] + [vmem] * 6 + [any_spec] * 4,
            out_specs=(vmem, any_spec, any_spec),
            scratch_shapes=[
                pltpu.VMEM(w_qkv.shape, BF16),
                pltpu.VMEM(k3.shape, BF16),
                pltpu.VMEM(v3.shape, BF16),
                pltpu.VMEM(w_out.shape, BF16),
                pltpu.VMEM((n_batch, n_q, head), F32),
                pltpu.VMEM((n_batch, n_q, head), F32),
                pltpu.VMEM((2, n_batch, head), F32),
                pltpu.VMEM((n_batch, n_q * head), BF16),
                dma((n_qkv,)), dma((n_batch // group,)), dma((n_batch // group,)), dma((1,)), dma((n_batch // group,)), dma((n_batch // group,)),
            ],
            compiler_params=pltpu.CompilerParams(vmem_limit_bytes=40 * 1024 * 1024),
            name='attention',
        )(seq_lens, hidden, rope_cos, rope_sin, ln1_scale, ln1_bias, b_qkv, w_qkv, k3, v3, w_out)

        n_cols = 4
        d_col = d_model // n_cols
        half = d_model // 2
        wg = jnp.swapaxes(w_gate, 1, 2)
        wu = jnp.swapaxes(w_up, 1, 2)
        n_exp, ff, _ = wg.shape
        n_all = w_router.shape[1]
        n_tok = n_ep * n_batch
        n_pair = n_exp // 2
        ids_t = expert_ids.T
        V = pltpu.VMEM
        m = max(n_tp, n_x)
        assert n_tp == n_x
        out = pl.pallas_call(
            functools.partial(moe_kernel, n_tp, n_x, n_cols),
            out_shape=jax.ShapeDtypeStruct((n_tp, rows, d_model), BF16),
            in_specs=[any_spec] * 10,
            out_specs=any_spec,
            scratch_shapes=[
                V((n_tp, rows, d_model), BF16), V((n_tp, rows, d_model), BF16), V(ids_t.shape, jnp.int32),
                V((d_model,), BF16), V((d_model,), BF16), V((d_model,), BF16), V(w_router.shape, BF16),
                V(wg.shape, BF16), V(wg.shape, BF16), V(wg.shape, BF16),
                V((n_tp, rows, n_all), F32),
                V((n_tp - 1, rows, d_model), BF16),
                V((rows, d_model), BF16),
                V((n_x, 2, n_tp, rows, half), BF16),
                V((n_x, 2, n_tp, rows, half + n_all), BF16),
                V((d_model, n_tok), BF16),
                V((n_all, n_tok), F32),
                V((n_pair, n_tok, 2 * ff), BF16),
                V((n_cols, n_x, 2, n_tp, rows, d_col), F32),
                V((n_cols, n_x, 2, n_tp, rows, d_col), BF16),
                V((n_cols, n_x, n_tp, rows, d_col), BF16),
                V((n_cols, n_x, n_tp, rows, d_col), BF16),
                V((n_cols, n_x, n_tp, rows, d_col), F32),
                V((n_cols, m - 1, m, rows, d_col), BF16),
                V((n_cols, m, rows, d_col), BF16),
                V((n_cols, m, rows, d_col), F32),
                V((n_cols, m - 1, rows, d_col), BF16),
                V((n_cols, n_tp, rows, d_col), BF16),
                dma((7,)), dma((3, n_pair)),
                dma((m - 1,)), dma((m - 1,)),
                dma((2, m - 1)), dma((2, m - 1)), dma((2, m - 1)), dma((2, m - 1)), dma((2, m)), dma((2, m)),
                dma((n_cols,)), dma((n_cols,)),
                dma((n_cols, m - 1)), dma((n_cols, m - 1)), dma((n_cols, m - 1)), dma((n_cols, m - 1)), dma((n_cols, m - 1)), dma((n_cols, m - 1)),
                dma((n_cols,)),
            ],
            compiler_params=pltpu.CompilerParams(vmem_limit_bytes=62 * 1024 * 1024, collective_id=0, has_side_effects=True),
            name='moe',
        )(part, hidden.reshape(n_tp, rows, d_model), ids_t, b_out, ln2_scale, ln2_bias, w_router, wg, wu, w_down)
        return out.reshape(n_batch, d_model), k_out.reshape(k_cache.shape), v_out.reshape(v_cache.shape)

    in_specs = (token_rows, token_vec, token_rows, token_rows, P(), P(), P(None, 'tp'), P('tp'), P('tp', None), P(), cache_spec, cache_spec, P(), P(), P(), token_rows, expert_in, expert_in, expert_down)
    return jax.shard_map(device_step, mesh=mesh, in_specs=in_specs, out_specs=(token_rows, cache_spec, cache_spec), check_vma=False)
```

time: 227 us -> 84.9 us (0.37)
  the two profiles are of different devices: /device:TPU:97 before, /device:TPU:96 now
where the time goes in v1:
time: 84.9 us; the launch traced here: 84.4 us
  Pallas kernels  68.7 us (81%)
  local copies, waits for them, and re-layouts  15.1 us (18%)
    pallas_call x1, Pallas kernels, device_step(): pl.pallas_call(functools.partial(moe_kernel, n_tp, n_x, n_cols), out_shap...  62.2 us
    unnamed x25, local copies, waits for them, and re-layouts  15.1 us
    pallas_call x1, Pallas kernels, device_step(): pl.pallas_call(functools.partial(attention_kernel, n_qkv, group), out_sha...  6.44 us

profile of v1, /device:TPU:96, one launch (start us, length us, event | category | flops | bytes accessed | tf_op | source)
XLA Modules:
  0.0 84.4 jit_solution(14169147950155879710)
XLA Ops:
  0.6 0.0 copy-start
  0.6 2.5 %copy-done = bf16[2048,1280]{1,0:T(8,128)(2,1)S(1)} copy-done((bf16[2048,1280]{1,0:T(8,128)(2,1)S(1)}, bf16[2048,1280]{1,0:T(8,128)(2,1)}, u32[]{:S(2)}) %copy-start) | copy-done | bytes 5242904
  3.1 0.0 copy-start.1
  3.1 2.2 %copy-done.1 = bf16[1024,2048]{1,0:T(8,128)(2,1)S(1)} copy-done((bf16[1024,2048]{1,0:T(8,128)(2,1)S(1)}, bf16[1024,2048]{1,0:T(8,128)(2,1)}, u32[]{:S(2)}) %copy-start.1) | copy-done | bytes 4194328
  5.3 0.0 copy-start.2
  5.3 1.6 %copy-done.2 = bf16[32,256,1,128]{3,1,2,0:T(8,128)(2,1)S(1)} copy-done((bf16[32,256,1,128]{3,1,2,0:T(8,128)(2,1)S(1)}, bf16[32,256,1,128]{3,1,2,0:T(8,128)(2,1)}, u32[]{:S(2)}) %copy-start.2) | copy-done | bytes 2097176
  6.9 0.0 copy-start.3
  6.9 1.6 %copy-done.3 = bf16[32,256,1,128]{3,1,2,0:T(8,128)(2,1)S(1)} copy-done((bf16[32,256,1,128]{3,1,2,0:T(8,128)(2,1)S(1)}, bf16[32,256,1,128]{3,1,2,0:T(8,128)(2,1)}, u32[]{:S(2)}) %copy-start.3) | copy-done | bytes 2097176
  8.5 0.0 copy-start.4
  8.5 0.9 %copy-done.4 = bf16[32,2048]{1,0:T(8,128)(2,1)S(1)} copy-done((bf16[32,2048]{1,0:T(8,128)(2,1)S(1)}, bf16[32,2048]{1,0:T(8,128)(2,1)}, u32[]{:S(2)}) %copy-start.4) | copy-done | bytes 131096
  9.4 0.0 copy-start.6
  9.4 0.7 copy-done.6
  10.1 0.0 copy-start.7
  10.1 0.7 copy-done.7
  10.8 0.0 copy-start.8
  10.8 0.7 copy-done.8
  11.5 0.0 copy-start.9
  11.5 0.7 copy-done.9
  12.2 0.0 copy-start.10
  12.2 0.7 copy-done.10
  12.9 0.0 copy-start.11
  12.9 0.7 copy-done.11
  13.6 6.4 %attention.1 = (bf16[4,8,2048]{2,1,0:T(8,128)(2,1)S(1)}, bf16[32,256,128]{2,1,0:T(8,128)(2,1)}, bf16[32,256,128]{2,1,0:T(8,128)(2,1)}) custom-call(s32[32]{0:T(128)S(1)} %copy-done.11, bf16[32,2048]{1,0:T(8,128)(2,1)S(1)} %copy-done.4, f32[32,64]{1,0:T(8,128)S(1)} %copy-done.6, f32[32,64]{1,0:T(8,128)S(1)} %copy-done.7, bf16[2048]{0:T(1024)(128)(2,1)S(1)} %copy-done.8, ...), custom_call_target="tpu_custom_call" | custom-call | tf_op jit(solution)/shard_map/attention/pallas_call | solution.py:353
  20.0 0.0 copy-start.5
  20.0 0.6 copy-done.5
  20.7 62.2 %moe.1 = bf16[4,8,2048]{2,1,0:T(8,128)(2,1)} custom-call(bf16[4,8,2048]{2,1,0:T(8,128)(2,1)} %copy-done.5, bf16[4,8,2048]{2,1,0:T(8,128)(2,1)} %bitcast.15, s32[8,32]{1,0:T(8,128)} %bitcast.19, bf16[2048]{0:T(1024)(128)(2,1)} %bout_hbm.1, bf16[2048]{0:T(1024)(128)(2,1)} %lns_hbm.1, bf16[2048]{0:T(1024)(128)(2,1)} %lnb_hbm.1, bf16[2048,128]{1,0:T(8,128)(2,1)} %wr_hbm.1, ...), custom_call_target="tpu_custom_call" | custom-call | tf_op jit(solution)/shard_map/moe/pallas_call | solution.py:386
  82.9 1.6 %copy.25 = bf16[32,2048]{1,0:T(8,128)(2,1)} copy(bf16[32,2048]{1,0:T(8,128)(2,1)} %bitcast.18) | data formatting | bytes 262144
Async XLA Ops:
  0.6 2.5 %copy-start = (bf16[2048,1280]{1,0:T(8,128)(2,1)S(1)}, bf16[2048,1280]{1,0:T(8,128)(2,1)}, u32[]{:S(2)}) copy-start(bf16[2048,1280]{1,0:T(8,128)(2,1)} %wqkv_hbm.1) | copy-start | bytes 15728644
  3.1 2.2 %copy-start.1 = (bf16[1024,2048]{1,0:T(8,128)(2,1)S(1)}, bf16[1024,2048]{1,0:T(8,128)(2,1)}, u32[]{:S(2)}) copy-start(bf16[1024,2048]{1,0:T(8,128)(2,1)} %wout_hbm.1) | copy-start | bytes 12582916
  5.3 1.6 %copy-start.2 = (bf16[32,256,1,128]{3,1,2,0:T(8,128)(2,1)S(1)}, bf16[32,256,1,128]{3,1,2,0:T(8,128)(2,1)}, u32[]{:S(2)}) copy-start(bf16[32,256,1,128]{3,1,2,0:T(8,128)(2,1)} %param.29) | copy-start | bytes 6291460
  6.9 1.6 %copy-start.3 = (bf16[32,256,1,128]{3,1,2,0:T(8,128)(2,1)S(1)}, bf16[32,256,1,128]{3,1,2,0:T(8,128)(2,1)}, u32[]{:S(2)}) copy-start(bf16[32,256,1,128]{3,1,2,0:T(8,128)(2,1)} %param.30) | copy-start | bytes 6291460
  8.5 0.9 %copy-start.4 = (bf16[32,2048]{1,0:T(8,128)(2,1)S(1)}, bf16[32,2048]{1,0:T(8,128)(2,1)}, u32[]{:S(2)}) copy-start(bf16[32,2048]{1,0:T(8,128)(2,1)} %hid_ref.1) | copy-start | bytes 393220
  9.4 0.7 copy-start.6
  10.1 0.7 copy-start.7
  10.8 0.7 copy-start.8
  11.5 0.7 copy-start.9
  12.2 0.7 copy-start.10
  12.9 0.7 copy-start.11
  20.0 0.7 copy-start.5

commit v2 on v1

--- a/solution.py
+++ b/solution.py
@@ -26,14 +26,18 @@
     return ref[...].astype(F32)[None, :]
 
 
-def attention_kernel(n_qkv, group, seq_ref, hid_ref, cos_ref, sin_ref, lns_ref, lnb_ref, bqkv_ref, wqkv_hbm, k_hbm, v_hbm, wout_hbm,
-                     part_ref, kout_hbm, vout_hbm,
-                     wqkv, kbuf, vbuf, wout, q_s, c_s, new_s, ctx, sem_w, sem_k, sem_v, sem_o, sem_ko, sem_vo):
+def attention_kernel(n_qkv, group, seq_hbm, hid_hbm, cos_hbm, sin_hbm, lns_hbm, lnb_hbm, bqkv_hbm, wqkv_hbm, k_hbm, v_hbm, wout_hbm,
+                     part_hbm, kout_hbm, vout_hbm,
+                     seq_ref, hid_ref, cos_ref, sin_ref, lns_ref, lnb_ref, bqkv_ref, part_ref, sem_s, wqkv, kbuf, vbuf, wout, q_s, c_s, new_s, ctx, sem_w, sem_k, sem_v, sem_o, sem_ko, sem_vo):
     n_batch, s_max, head = kbuf.shape
     n_q = q_s.shape[1]
     d_model = wqkv.shape[0]
     n_groups = n_batch // group
     step = d_model // n_qkv
+    small = [(hid_hbm, hid_ref), (lns_hbm, lns_ref), (lnb_hbm, lnb_ref), (bqkv_hbm, bqkv_ref), (cos_hbm, cos_ref), (sin_hbm, sin_ref), (seq_hbm, seq_ref)]
+    small = [pltpu.make_async_copy(src, dst, sem_s.at[i]) for i, (src, dst) in enumerate(small)]
+    for cp in small:
+        cp.start()
     for i in range(n_qkv):
         rows = pl.ds(i * step, step)
         pltpu.make_async_copy(wqkv_hbm.at[rows], wqkv.at[rows], sem_w.at[i]).start()
@@ -43,6 +47,8 @@
         pltpu.make_async_copy(v_hbm.at[rows], vbuf.at[rows], sem_v.at[g]).start()
     pltpu.make_async_copy(wout_hbm, wout, sem_o.at[0]).start()
 
+    for cp in small:
+        cp.wait()
     normed = row_norm(hid_ref[...].astype(F32), row_of(lns_ref), row_of(lnb_ref))
     acc = jnp.broadcast_to(row_of(bqkv_ref), (n_batch, wqkv.shape[1]))
     total = None
@@ -100,10 +106,13 @@
     pltpu.make_async_copy(wout_hbm, wout, sem_o.at[0]).wait()
     part = jnp.dot(ctx[...], wout[...], preferred_element_type=F32)
     part_ref[...] = part.reshape(part_ref.shape).astype(BF16)
+    out_copy = pltpu.make_async_copy(part_ref, part_hbm, sem_s.at[0])
+    out_copy.start()
     for g in range(n_groups):
         rows = pl.ds(g * group, group)
         pltpu.make_async_copy(kbuf.at[rows], kout_hbm.at[rows], sem_ko.at[g]).wait()
         pltpu.make_async_copy(vbuf.at[rows], vout_hbm.at[rows], sem_vo.at[g]).wait()
+    out_copy.wait()
 
 
 def moe_kernel(n_tp, n_x, n_cols, part_hbm, hid_hbm, ids_hbm, bout_hbm, lns_hbm, lnb_hbm, wr_hbm, wg_hbm, wu_hbm, wd_hbm,
@@ -151,12 +160,6 @@
         rows = pl.ds(2 * p, 2)
         return pltpu.make_async_copy(src.at[rows], dst.at[rows], sem_w.at[w, p])
 
-    for p in range(n_pair):
-        wcopy(0, p).start()
-        wcopy(1, p).start()
-    for p in range(n_pair):
-        wcopy(2, p).start()
-
     barrier = pltpu.get_barrier_semaphore()
     for dt in range(1, n_tp):
         pl.semaphore_signal(barrier, inc=1, device_id=y_peer(dt), device_id_type=MESH)
@@ -165,6 +168,11 @@
     pl.semaphore_signal(barrier, inc=1, device_id=partner, device_id_type=MESH)
     for cp in copies:
         cp.wait()
+    for p in range(n_pair):
+        wcopy(0, p).start()
+        wcopy(1, p).start()
+    for p in range(n_pair):
+        wcopy(2, p).start()
     pl.semaphore_wait(barrier, n_tp + n_x - 1)
 
     a_send = []
@@ -245,10 +253,10 @@
         g0 = g_t[pl.ds(e * n_exp + 2 * p, 1), :]
         g1 = g_t[pl.ds(e * n_exp + 2 * p + 1, 1), :]
         a = jnp.concatenate([a[:ff] * g0, a[ff:] * g1], axis=0)
-        act[p] = a.T.astype(BF16)
+        act[:, pl.ds(pl.multiple_of(2 * ff * p, 2 * ff), 2 * ff)] = a.T.astype(BF16)
         return carry
 
-    lax.fori_loop(0, n_pair, one_pair, 0)
+    lax.fori_loop(0, n_pair, one_pair, 0, unroll=2)
     for p in range(n_pair):
         wcopy(2, p).wait()
 
@@ -261,60 +269,60 @@
         return cp
 
     c0, c1, c2, dd = {}, {}, {}, {}
+    d_half = d_col // 2
 
     def down(j):
         cols = slice(j * d_col, (j + 1) * d_col)
-        o = None
-        for p in range(n_pair):
-            one = jnp.dot(act[p], wd[2 * p:2 * p + 2, :, cols].reshape(2 * ff, d_col), preferred_element_type=F32)
-            o = one if o is None else o + one
-        o = o.reshape(n_x, 2, n_tp, n_tok // (2 * n_x * n_tp), d_col)
-        o32[j] = o
-        c0_send[j] = o.astype(BF16)
-        c0[j] = csend(c0_send.at[j, :, 1 - c], c0_recv.at[j], c0_ss.at[j], c0_rs.at[j], partner)
+        o = jnp.dot(act[...], wd[:, :, cols].reshape(n_exp * ff, d_col), preferred_element_type=F32)
+        for h in range(2):
+            piece = o[:, h * d_half:(h + 1) * d_half].reshape(n_x, 2, n_tp, n_tok // (2 * n_x * n_tp), d_half)
+            o32[j, h] = piece
+            c0_send[j, h] = piece.astype(BF16)
+        c0[j] = csend(c0_send.at[j, :, :, 1 - c], c0_recv.at[j], c0_ss.at[j], c0_rs.at[j], partner)
+
+    def x_send(src, dst, ss, rs, j, h):
+        return [csend(src(x_dst(dx)), dst.at[j, h, dx - 1], ss.at[j, h, dx - 1], rs.at[j, h, dx - 1], x_peer(dx)) for dx in range(1, n_x)]
+
+    def y_send(src, dst, ss, rs, j, h):
+        return [csend(src(lax.rem(t + dt, n_tp)), dst.at[j, h, dt - 1], ss.at[j, h, dt - 1], rs.at[j, h, dt - 1], y_peer(dt)) for dt in range(1, n_tp)]
 
     def stage1(j):
         c0[j].wait_recv()
-        s = o32[j, :, c] + c0_recv[j].astype(F32)
-        c1_send[j] = s.astype(BF16)
-        c1_own[j] = s
-        if j < n_cols // 2:
-            c1[j] = [csend(c1_send.at[j, x_dst(dx)], c1_recv.at[j, dx - 1], c1_ss.at[j, dx - 1], c1_rs.at[j, dx - 1], x_peer(dx)) for dx in range(1, n_x)]
-        else:
-            c1[j] = [csend(c1_send.at[j, :, lax.rem(t + dt, n_tp)], c1_recv.at[j, dt - 1], c1_ss.at[j, dt - 1], c1_rs.at[j, dt - 1], y_peer(dt)) for dt in range(1, n_tp)]
+        for h in range(2):
+            s = o32[j, h, :, c] + c0_recv[j, h].astype(F32)
+            c1_send[j, h] = s.astype(BF16)
+            c1_own[j, h] = s
+        c1[j, 0] = x_send(lambda i: c1_send.at[j, 0, i], c1_recv, c1_ss, c1_rs, j, 0)
+        c1[j, 1] = y_send(lambda i: c1_send.at[j, 1, :, i], c1_recv, c1_ss, c1_rs, j, 1)
 
     def stage2(j):
-        for cp in c1[j]:
-            cp.wait_recv()
-        s = c1_own[j, x] if j < n_cols // 2 else c1_own[j, :, t]
-        for i in range(len(c1[j])):
-            s = s + c1_recv[j, i].astype(F32)
-        c2_send[j] = s.astype(BF16)
-        c2_own[j] = s
-        if j < n_cols // 2:
-            c2[j] = [csend(c2_send.at[j, lax.rem(t + dt, n_tp)], c2_recv.at[j, dt - 1], c2_ss.at[j, dt - 1], c2_rs.at[j, dt - 1], y_peer(dt)) for dt in range(1, n_tp)]
-        else:
-            c2[j] = [csend(c2_send.at[j, x_dst(dx)], c2_recv.at[j, dx - 1], c2_ss.at[j, dx - 1], c2_rs.at[j, dx - 1], x_peer(dx)) for dx in range(1, n_x)]
+        for h in range(2):
+            for cp in c1[j, h]:
+                cp.wait_recv()
+            s = c1_own[j, 1, :, t] if h else c1_own[j, 0, x]
+            for i in range(len(c1[j, h])):
+                s = s + c1_recv[j, h, i].astype(F32)
+            c2_send[j, h] = s.astype(BF16)
+            c2_own[j, h] = s
+            if h:
+                c2[j, 1] = x_send(lambda i: c2_send.at[j, 1, i], c2_recv, c2_ss, c2_rs, j, 1)
+            else:
+                c2[j, 0] = y_send(lambda i: c2_send.at[j, 0, i], c2_recv, c2_ss, c2_rs, j, 0)
 
     def stage3(j):
-        for cp in c2[j]:
-            cp.wait_recv()
-        s = c2_own[j, t] if j < n_cols // 2 else c2_own[j, x]
-        for i in range(len(c2[j])):
-            s = s + c2_recv[j, i].astype(F32)
-        cols = slice(j * d_col, (j + 1) * d_col)
-        outbuf[j, t] = (x1_s[:, cols].astype(F32) + s).astype(BF16)
+        for h in range(2):
+            for cp in c2[j, h]:
+                cp.wait_recv()
+            s = c2_own[j, 1, x] if h else c2_own[j, 0, t]
+            for i in range(len(c2[j, h])):
+                s = s + c2_recv[j, h, i].astype(F32)
+            cols = slice(j * d_col + h * d_half, j * d_col + (h + 1) * d_half)
+            outbuf[j, t, :, h * d_half:(h + 1) * d_half] = (x1_s[:, cols].astype(F32) + s).astype(BF16)
         dd[j] = [csend(outbuf.at[j, t], outbuf.at[j, t], d_ss.at[j, dt - 1], d_rs.at[j, dt - 1], y_peer(dt)) for dt in range(1, n_tp)]
 
-    for j in range(n_cols + 3):
-        if j < n_cols:
-            down(j)
-        if 0 <= j - 1 < n_cols:
-            stage1(j - 1)
-        if 0 <= j - 2 < n_cols:
-            stage2(j - 2)
-        if 0 <= j - 3 < n_cols:
-            stage3(j - 3)
+    plan = [(stage, j, pos) for j in range(n_cols) for stage, pos in ((down, j), (stage1, j + 1.25 if j < n_cols - 1 else j + 0.5), (stage2, j + 3.5), (stage3, j + 5.75))]
+    for stage, j, _ in sorted(plan, key=lambda one: one[2]):
+        stage(j)
     outs = []
     for j in range(n_cols):
         for cp in dd[j]:
@@ -337,9 +345,7 @@
     cache_spec = P(('dp', 'ep'), None, 'tp', None)
     expert_in = P('ep', None, 'tp')
     expert_down = P('ep', 'tp', None)
-    any_spec = pl.BlockSpec(memory_space=pl.ANY)
-    vmem = pl.BlockSpec(memory_space=pltpu.VMEM)
-    smem = pl.BlockSpec(memory_space=pltpu.SMEM)
+    hbm_spec = pl.BlockSpec(memory_space=pltpu.HBM)
 
     def device_step(hidden, seq_lens, rope_cos, rope_sin, ln1_scale, ln1_bias, w_qkv, b_qkv, w_out, b_out, k_cache, v_cache, ln2_scale, ln2_bias, w_router, expert_ids, w_gate, w_up, w_down):
         n_batch, d_model = hidden.shape
@@ -353,9 +359,18 @@
         part, k_out, v_out = pl.pallas_call(
             functools.partial(attention_kernel, n_qkv, group),
             out_shape=(jax.ShapeDtypeStruct((n_tp, rows, d_model), BF16), jax.ShapeDtypeStruct(k3.shape, BF16), jax.ShapeDtypeStruct(v3.shape, BF16)),
-            in_specs=[smem] + [vmem] * 6 + [any_spec] * 4,
-            out_specs=(vmem, any_spec, any_spec),
+            in_specs=[hbm_spec] * 11,
+            out_specs=(hbm_spec,) * 3,
             scratch_shapes=[
+                pltpu.SMEM(seq_lens.shape, jnp.int32),
+                pltpu.VMEM(hidden.shape, BF16),
+                pltpu.VMEM(rope_cos.shape, F32),
+                pltpu.VMEM(rope_sin.shape, F32),
+                pltpu.VMEM((d_model,), BF16),
+                pltpu.VMEM((d_model,), BF16),
+                pltpu.VMEM(b_qkv.shape, BF16),
+                pltpu.VMEM((n_tp, rows, d_model), BF16),
+                dma((7,)),
                 pltpu.VMEM(w_qkv.shape, BF16),
                 pltpu.VMEM(k3.shape, BF16),
                 pltpu.VMEM(v3.shape, BF16),
@@ -366,12 +381,13 @@
                 pltpu.VMEM((n_batch, n_q * head), BF16),
                 dma((n_qkv,)), dma((n_batch // group,)), dma((n_batch // group,)), dma((1,)), dma((n_batch // group,)), dma((n_batch // group,)),
             ],
-            compiler_params=pltpu.CompilerParams(vmem_limit_bytes=40 * 1024 * 1024),
+            compiler_params=pltpu.CompilerParams(vmem_limit_bytes=63 * 1024 * 1024),
             name='attention',
         )(seq_lens, hidden, rope_cos, rope_sin, ln1_scale, ln1_bias, b_qkv, w_qkv, k3, v3, w_out)
 
         n_cols = 4
         d_col = d_model // n_cols
+        d_half = d_col // 2
         half = d_model // 2
         wg = jnp.swapaxes(w_gate, 1, 2)
         wu = jnp.swapaxes(w_up, 1, 2)
@@ -386,8 +402,8 @@
         out = pl.pallas_call(
             functools.partial(moe_kernel, n_tp, n_x, n_cols),
             out_shape=jax.ShapeDtypeStruct((n_tp, rows, d_model), BF16),
-            in_specs=[any_spec] * 10,
-            out_specs=any_spec,
+            in_specs=[hbm_spec] * 10,
+            out_specs=hbm_spec,
             scratch_shapes=[
                 V((n_tp, rows, d_model), BF16), V((n_tp, rows, d_model), BF16), V(ids_t.shape, jnp.int32),
                 V((d_model,), BF16), V((d_model,), BF16), V((d_model,), BF16), V(w_router.shape, BF16),
@@ -399,25 +415,25 @@
                 V((n_x, 2, n_tp, rows, half + n_all), BF16),
                 V((d_model, n_tok), BF16),
                 V((n_all, n_tok), F32),
-                V((n_pair, n_tok, 2 * ff), BF16),
-                V((n_cols, n_x, 2, n_tp, rows, d_col), F32),
-                V((n_cols, n_x, 2, n_tp, rows, d_col), BF16),
-                V((n_cols, n_x, n_tp, rows, d_col), BF16),
-                V((n_cols, n_x, n_tp, rows, d_col), BF16),
-                V((n_cols, n_x, n_tp, rows, d_col), F32),
-                V((n_cols, m - 1, m, rows, d_col), BF16),
-                V((n_cols, m, rows, d_col), BF16),
-                V((n_cols, m, rows, d_col), F32),
-                V((n_cols, m - 1, rows, d_col), BF16),
+                V((n_tok, n_exp * ff), BF16),
+                V((n_cols, 2, n_x, 2, n_tp, rows, d_half), F32),
+                V((n_cols, 2, n_x, 2, n_tp, rows, d_half), BF16),
+                V((n_cols, 2, n_x, n_tp, rows, d_half), BF16),
+                V((n_cols, 2, n_x, n_tp, rows, d_half), BF16),
+                V((n_cols, 2, n_x, n_tp, rows, d_half), F32),
+                V((n_cols, 2, m - 1, m, rows, d_half), BF16),
+                V((n_cols, 2, m, rows, d_half), BF16),
+                V((n_cols, 2, m, rows, d_half), F32),
+                V((n_cols, 2, m - 1, rows, d_half), BF16),
                 V((n_cols, n_tp, rows, d_col), BF16),
                 dma((7,)), dma((3, n_pair)),
                 dma((m - 1,)), dma((m - 1,)),
                 dma((2, m - 1)), dma((2, m - 1)), dma((2, m - 1)), dma((2, m - 1)), dma((2, m)), dma((2, m)),
                 dma((n_cols,)), dma((n_cols,)),
-                dma((n_cols, m - 1)), dma((n_cols, m - 1)), dma((n_cols, m - 1)), dma((n_cols, m - 1)), dma((n_cols, m - 1)), dma((n_cols, m - 1)),
+                dma((n_cols, 2, m - 1)), dma((n_cols, 2, m - 1)), dma((n_cols, 2, m - 1)), dma((n_cols, 2, m - 1)), dma((n_cols, m - 1)), dma((n_cols, m - 1)),
                 dma((n_cols,)),
             ],
-            compiler_params=pltpu.CompilerParams(vmem_limit_bytes=62 * 1024 * 1024, collective_id=0, has_side_effects=True),
+            compiler_params=pltpu.CompilerParams(vmem_limit_bytes=63 * 1024 * 1024, collective_id=0, has_side_effects=True),
             name='moe',
         )(part, hidden.reshape(n_tp, rows, d_model), ids_t, b_out, ln2_scale, ln2_bias, w_router, wg, wu, w_down)
         return out.reshape(n_batch, d_model), k_out.reshape(k_cache.shape), v_out.reshape(v_cache.shape)

time: 84.9 us -> 58.6 us (0.69)
  local copies, waits for them, and re-layouts: 15.1 us -> 1.57 us
  Pallas kernels: 68.7 us -> 56.3 us
    pallas_call x1, Pallas kernels: 62.2 us -> 48.1 us  [device_step(): pl.pallas_call(functools.partial(moe_kernel, n_tp, n_x, n_cols), out_shap...]
    unnamed x25 -> x1, local copies, waits for them, and re-layouts: 15.1 us -> 1.57 us
    pallas_call x1, Pallas kernels: 6.44 us -> 8.21 us  [device_step(): pl.pallas_call(functools.partial(attention_kernel, n_qkv, group), out_sha...]
where the time goes in v2:
time: 58.6 us; the launch traced here: 58.5 us
  Pallas kernels  56.3 us (96%)
  local copies, waits for them, and re-layouts  1.57 us (3%)
  between operations  0.65 us (1%)
    pallas_call x1, Pallas kernels, device_step(): pl.pallas_call(functools.partial(moe_kernel, n_tp, n_x, n_cols), out_shap...  48.1 us
    pallas_call x1, Pallas kernels, device_step(): pl.pallas_call(functools.partial(attention_kernel, n_qkv, group), out_sha...  8.21 us
    unnamed x1, local copies, waits for them, and re-layouts  1.57 us

profile of v2, /device:TPU:96, one launch (start us, length us, event | category | flops | bytes accessed | tf_op | source)
XLA Modules:
  0.0 58.5 jit_solution(9573344794859806282)
XLA Ops:
  0.6 8.2 %attention.1 = (bf16[4,8,2048]{2,1,0:T(8,128)(2,1)}, bf16[32,256,128]{2,1,0:T(8,128)(2,1)}, bf16[32,256,128]{2,1,0:T(8,128)(2,1)}) custom-call(s32[32]{0:T(128)} %seq_hbm.1, bf16[32,2048]{1,0:T(8,128)(2,1)} %hid_hbm.1, f32[32,64]{1,0:T(8,128)} %cos_hbm.1, f32[32,64]{1,0:T(8,128)} %sin_hbm.1, bf16[2048]{0:T(1024)(128)(2,1)} %lns_hbm.2, ...), custom_call_target="tpu_custom_call" | custom-call | tf_op jit(solution)/shard_map/attention/pallas_call | solution.py:359
  8.9 48.1 %moe.1 = bf16[4,8,2048]{2,1,0:T(8,128)(2,1)} custom-call(bf16[4,8,2048]{2,1,0:T(8,128)(2,1)} %get-tuple-element.6.part_hbm, bf16[4,8,2048]{2,1,0:T(8,128)(2,1)} %bitcast.17, s32[8,32]{1,0:T(8,128)} %bitcast.19, bf16[2048]{0:T(1024)(128)(2,1)} %bout_hbm.1, bf16[2048]{0:T(1024)(128)(2,1)} %lns_hbm.3, bf16[2048]{0:T(1024)(128)(2,1)} %lnb_hbm.3, ...), custom_call_target="tpu_custom_call" | custom-call | tf_op jit(solution)/shard_map/moe/pallas_call | solution.py:402
  56.9 1.6 %copy.25 = bf16[32,2048]{1,0:T(8,128)(2,1)} copy(bf16[32,2048]{1,0:T(8,128)(2,1)} %bitcast.18) | data formatting | bytes 262144

commit v3 on v2

v3 whole, which is shorter than its diff:
```python
import functools

import jax
import jax.numpy as jnp
from jax import lax
from jax.experimental import pallas as pl
from jax.experimental.pallas import tpu as pltpu
from jax.sharding import PartitionSpec as P

EPS = 1e-5
F32 = jnp.float32
BF16 = jnp.bfloat16
MESH = pl.DeviceIdType.MESH
NT = (((1,), (1,)), ((), ()))


def row_norm(vals_f32, ln_scale, ln_bias):
    row_mean = jnp.mean(vals_f32, axis=-1, keepdims=True)
    centered = vals_f32 - row_mean
    row_var = jnp.mean(centered * centered, axis=-1, keepdims=True)
    normed = centered * lax.rsqrt(row_var + EPS)
    return (normed * ln_scale + ln_bias).astype(BF16)


def row_of(ref):
    return ref[...].astype(F32)[None, :]


def attention_kernel(n_qkv, group, seq_hbm, hid_hbm, cos_hbm, sin_hbm, lns_hbm, lnb_hbm, bqkv_hbm, wqkv_hbm, k_hbm, v_hbm,
                     ctx_hbm, kout_hbm, vout_hbm,
                     seq_ref, hid_ref, cos_ref, sin_ref, lns_ref, lnb_ref, bqkv_ref, sem_s, wqkv, kbuf, vbuf, q_s, c_s, new_s, ctx, sem_w, sem_k, sem_v, sem_ko, sem_vo):
    n_batch, s_max, head = kbuf.shape
    n_q = q_s.shape[1]
    d_model = wqkv.shape[0]
    n_groups = n_batch // group
    step = d_model // n_qkv
    small = [(hid_hbm, hid_ref), (lns_hbm, lns_ref), (lnb_hbm, lnb_ref), (bqkv_hbm, bqkv_ref), (cos_hbm, cos_ref), (sin_hbm, sin_ref), (seq_hbm, seq_ref)]
    small = [pltpu.make_async_copy(src, dst, sem_s.at[i]) for i, (src, dst) in enumerate(small)]
    for cp in small:
        cp.start()
    for i in range(n_qkv):
        rows = pl.ds(i * step, step)
        pltpu.make_async_copy(wqkv_hbm.at[rows], wqkv.at[rows], sem_w.at[i]).start()

    for cp in small:
        cp.wait()
    for g in range(n_groups):
        rows = pl.ds(g * group, group)
        pltpu.make_async_copy(k_hbm.at[rows], kbuf.at[rows], sem_k.at[g]).start()
        pltpu.make_async_copy(v_hbm.at[rows], vbuf.at[rows], sem_v.at[g]).start()
    normed = row_norm(hid_ref[...].astype(F32), row_of(lns_ref), row_of(lnb_ref))
    acc = jnp.broadcast_to(row_of(bqkv_ref), (n_batch, wqkv.shape[1]))
    total = None
    for i in range(n_qkv):
        rows = pl.ds(i * step, step)
        pltpu.make_async_copy(wqkv_hbm.at[rows], wqkv.at[rows], sem_w.at[i]).wait()
        one = jnp.dot(normed[:, i * step:(i + 1) * step], wqkv[rows, :], preferred_element_type=F32)
        total = one if total is None else total + one
    qkv = (total + acc).astype(BF16).astype(F32)
    cos = jnp.concatenate([cos_ref[...], cos_ref[...]], axis=-1)
    sin = jnp.concatenate([-sin_ref[...], sin_ref[...]], axis=-1)
    for j in range(n_q + 1):
        x = qkv[:, j * head:(j + 1) * head]
        rot = x * cos + pltpu.roll(x, head // 2, 1) * sin
        if j < n_q:
            q_s[:, j, :] = rot
        else:
            new_s[0] = rot
    new_s[1] = qkv[:, (n_q + 1) * head:]

    row_iota = lax.broadcasted_iota(jnp.int32, (16, head), 0)
    lane_iota = lax.broadcasted_iota(jnp.int32, (n_q, s_max), 1)

    def one_group(g, carry):
        rows = pl.ds(g * group, group)
        pltpu.make_async_copy(k_hbm.at[rows], kbuf.at[rows], sem_k.at[g]).wait()
        pltpu.make_async_copy(v_hbm.at[rows], vbuf.at[rows], sem_v.at[g]).wait()
        scores = []
        for i in range(group):
            b = g * group + i
            p = seq_ref[b]
            base = pl.multiple_of((p // 16) * 16, 16)
            hit = row_iota == (p - base)
            for buf, which in ((kbuf, 0), (vbuf, 1)):
                old = buf[b, pl.ds(base, 16), :].astype(F32)
                row = new_s[which, pl.ds(b, 1), :]
                buf[b, pl.ds(base, 16), :] = jnp.where(hit, row, old).astype(BF16)
        pltpu.make_async_copy(kbuf.at[rows], kout_hbm.at[rows], sem_ko.at[g]).start()
        pltpu.make_async_copy(vbuf.at[rows], vout_hbm.at[rows], sem_vo.at[g]).start()
        for i in range(group):
            b = g * group + i
            s = lax.dot_general(q_s[b].astype(BF16), kbuf[b], NT, preferred_element_type=F32) * head ** -0.5
            scores.append(jnp.where(lane_iota <= seq_ref[b], s, -jnp.inf))
        s = jnp.concatenate(scores, axis=0)
        e = jnp.exp(s - jnp.max(s, axis=-1, keepdims=True))
        probs = (e / jnp.sum(e, axis=-1, keepdims=True))
        for i in range(group):
            b = g * group + i
            c_s[b] = jnp.dot(probs[i * n_q:(i + 1) * n_q].astype(BF16), vbuf[b], preferred_element_type=F32)
        return carry

    lax.fori_loop(0, n_groups, one_group, 0)
    for j in range(n_q):
        ctx[:, j * head:(j + 1) * head] = c_s[:, j, :].astype(BF16)
    out_copy = pltpu.make_async_copy(ctx, ctx_hbm, sem_s.at[0])
    out_copy.start()
    for g in range(n_groups):
        rows = pl.ds(g * group, group)
        pltpu.make_async_copy(kbuf.at[rows], kout_hbm.at[rows], sem_ko.at[g]).wait()
        pltpu.make_async_copy(vbuf.at[rows], vout_hbm.at[rows], sem_vo.at[g]).wait()
    out_copy.wait()


def moe_kernel(n_tp, n_x, widths, ctx_hbm, hid_hbm, ids_hbm, bout_hbm, lns_hbm, lnb_hbm, wout_hbm, wr_hbm, wg_hbm, wu_hbm, wd_hbm,
               out_hbm,
               ctx, hid, ids, bout, lns, lnb, wout, wr, wg, wu, wd, mask_s, part, a_recv, x1_s, ga, gb, h_s, acc, act, outbuf, cbufs,
               sem_in, sem_o, sem_w, a_ss, a_rs, b1_ss, b1_rs, b2_ss, b2_rs, b3_ss, b3_rs, x_ss, x_rs,
               c0_ss, c0_rs, c1_ss, c1_rs, c2_ss, c2_rs, sem_out):
    t = lax.axis_index('tp')
    e = lax.axis_index('ep')
    x = e // 2
    c = e % 2
    n_exp, ff, d_model = wg.shape
    n_all = wr.shape[1]
    rows = x1_s.shape[1]
    n_tok = h_s.shape[0]
    n_k, quarter = ga.shape[0], ga.shape[-1]
    k_cols = 2 * quarter
    n_cols = len(widths)
    starts = [sum(widths[:j]) for j in range(n_cols)]

    def y_dst(dt):
        return lax.rem(t + dt, n_tp)

    def y_peer(dt):
        return {'tp': y_dst(dt)}

    def y_src(dt):
        return lax.rem(t + n_tp - dt, n_tp)

    def x_dst(dx):
        return lax.rem(x + dx, n_x)

    def x_peer(dx):
        return {'ep': 2 * x_dst(dx) + c}

    def x_src(dx):
        return lax.rem(x + n_x - dx, n_x)

    partner = {'ep': 2 * x + 1 - c}
    sent = []

    def send(src, dst, ss, rs, dev):
        cp = pltpu.make_async_remote_copy(src_ref=src, dst_ref=dst, send_sem=ss, recv_sem=rs, device_id=dev, device_id_type=MESH)
        cp.start()
        sent.append(cp)
        return cp

    small = [(ctx_hbm, ctx), (ids_hbm, ids), (hid_hbm.at[t], hid), (bout_hbm, bout), (lns_hbm, lns), (lnb_hbm, lnb)]
    copies = [pltpu.make_async_copy(src, dst, sem_in.at[i]) for i, (src, dst) in enumerate(small)]
    for cp in copies:
        cp.start()
    n_o = part.shape[0]
    o_cols = d_model // n_o
    o_copies = [pltpu.make_async_copy(wout_hbm.at[:, pl.ds(i * o_cols, o_cols)], wout.at[:, pl.ds(i * o_cols, o_cols)], sem_o.at[i]) for i in range(n_o)]
    for cp in o_copies:
        cp.start()
    r_copy = pltpu.make_async_copy(wr_hbm, wr, sem_in.at[len(small)])
    r_copy.start()

    barrier = pltpu.get_barrier_semaphore()
    for dt in range(1, n_tp):
        pl.semaphore_signal(barrier, inc=1, device_id=y_peer(dt), device_id_type=MESH)
    for dx in range(1, n_x):
        pl.semaphore_signal(barrier, inc=1, device_id=x_peer(dx), device_id_type=MESH)
    pl.semaphore_signal(barrier, inc=1, device_id=partner, device_id_type=MESH)
    n_pair = n_exp // 2

    def wcopy(w, p):
        src, dst = ((wg_hbm, wg), (wu_hbm, wu), (wd_hbm, wd))[w]
        pair = pl.ds(2 * p, 2)
        return pltpu.make_async_copy(src.at[pair], dst.at[pair], sem_w.at[w, p])

    for cp in copies:
        cp.wait()
    exp_iota = lax.broadcasted_iota(jnp.int32, (n_all, ids.shape[1]), 0)
    picked = jnp.zeros((n_all, ids.shape[1]), F32)
    for k in range(ids.shape[0]):
        picked = picked + jnp.where(exp_iota == ids[k:k + 1, :], 1.0, 0.0)
    mask_s[...] = picked.T.reshape(mask_s.shape)
    pl.semaphore_wait(barrier, n_tp + n_x - 1)
    a = []
    for i in range(n_o):
        o_copies[i].wait()
        if i == n_o - 1:
            r_copy.wait()
            for p in range(n_pair):
                wcopy(0, p).start()
                wcopy(1, p).start()
            for p in range(n_pair):
                wcopy(2, p).start()
        o = jnp.dot(ctx[...], wout[:, i * o_cols:(i + 1) * o_cols], preferred_element_type=F32)
        part[i] = o.reshape(n_tp, rows, o_cols).astype(BF16)
        a.append([send(part.at[i, y_dst(dt)], a_recv.at[i, dt - 1], a_ss.at[i, dt - 1], a_rs.at[i, dt - 1], y_peer(dt)) for dt in range(1, n_tp)])
    sums = []
    for i in range(n_o):
        total = part[i, t].astype(F32)
        for dt in range(1, n_tp):
            a[i][dt - 1].wait_recv()
            total = total + a_recv[i, dt - 1].astype(F32)
        sums.append(total)
    x1 = (hid[...].astype(F32) + jnp.concatenate(sums, axis=-1) + row_of(bout)).astype(BF16)
    x1_s[t] = x1
    h2 = row_norm(x1.astype(F32), row_of(lns), row_of(lnb))
    b1, b2, b3 = {}, {}, {}

    def first(k):
        lo = k * k_cols
        ga[k, x, c, t] = h2[:, lo:lo + quarter]
        gb[k, x, c, t, :, 0:quarter] = h2[:, lo + quarter:lo + k_cols]
        b1[k, 0] = [send(ga.at[k, x, c, t], ga.at[k, x, c, t], b1_ss.at[k, 0, dt - 1], b1_rs.at[k, 0, dt - 1], y_peer(dt)) for dt in range(1, n_tp)]
        b1[k, 1] = [send(gb.at[k, x, c, t], gb.at[k, x, c, t], b1_ss.at[k, 1, dx - 1], b1_rs.at[k, 1, dx - 1], x_peer(dx)) for dx in range(1, n_x)]

    def second(k):
        for cp in b1[k, 0]:
            cp.wait_recv()
        b2[k, 0] = [send(ga.at[k, x, c], ga.at[k, x, c], b2_ss.at[k, 0, dx - 1], b2_rs.at[k, 0, dx - 1], x_peer(dx)) for dx in range(1, n_x)]
        for cp in b1[k, 1]:
            cp.wait_recv()
        b2[k, 1] = [send(gb.at[k, :, c, t], gb.at[k, :, c, t], b2_ss.at[k, 1, dt - 1], b2_rs.at[k, 1, dt - 1], y_peer(dt)) for dt in range(1, n_tp)]
        b3[k] = [send(ga.at[k, x, c], ga.at[k, x, c], b3_ss.at[k, 0, 0], b3_rs.at[k, 0, 0], partner), send(gb.at[k, :, c, t], gb.at[k, :, c, t], b3_ss.at[k, 1, 0], b3_rs.at[k, 1, 0], partner)]

    def third(k):
        for d in range(1, n_x):
            b2[k, 0][d - 1].wait_recv()
            xs = x_src(d)
            b3[k].append(send(ga.at[k, xs, c], ga.at[k, xs, c], b3_ss.at[k, 0, d], b3_rs.at[k, 0, d], partner))
            b2[k, 1][d - 1].wait_recv()
            ts = y_src(d)
            b3[k].append(send(gb.at[k, :, c, ts], gb.at[k, :, c, ts], b3_ss.at[k, 1, d], b3_rs.at[k, 1, d], partner))

    def gathered(k):
        for cp in b3[k]:
            cp.wait_recv()
        lo = k * k_cols
        for h, ref in ((0, ga), (1, gb)):
            h_s[:, lo + h * quarter:lo + (h + 1) * quarter] = ref[k, :, :, :, :, 0:quarter].astype(F32).reshape(n_tok, quarter).astype(BF16)

    for k in range(n_k - 1):
        first(k)
    logits = jnp.dot(h2, wr[...], preferred_element_type=F32)
    logits = jnp.where(mask_s[t] > 0.5, logits, -jnp.inf)
    ex = jnp.exp(logits - jnp.max(logits, axis=-1, keepdims=True))
    gb[n_k - 1, x, c, t, :, quarter:quarter + n_all] = (ex / jnp.sum(ex, axis=-1, keepdims=True)).astype(BF16)
    first(n_k - 1)
    for k in range(n_k):
        second(k)
    x1_sends = [send(x1_s.at[t], x1_s.at[t], x_ss.at[dt - 1], x_rs.at[dt - 1], y_peer(dt)) for dt in range(1, n_tp)]
    third(0)
    quad = 8
    wide = quad * ff

    def product(w, q, lo, hi):
        return lax.dot_general(h_s[:, lo:hi], w[q * quad:(q + 1) * quad, :, lo:hi].reshape(wide, hi - lo), NT, preferred_element_type=F32)

    lane = lax.broadcasted_iota(jnp.int32, (n_tok, 128), 1)
    for k in range(n_k):
        gathered(k)
        lo, hi = k * k_cols, (k + 1) * k_cols
        if k == n_k - 1:
            gates = gb[k, :, :, :, :, quarter:quarter + n_all].astype(F32).reshape(n_tok, n_all)
            gates = pltpu.roll(gates, lax.rem(n_all - e * n_exp, n_all), 1)
        for q in range(n_exp // quad):
            if k == 0:
                for p in range(q * quad // 2, (q + 1) * quad // 2):
                    wcopy(0, p).wait()
                    wcopy(1, p).wait()
            cols = slice(q * wide, (q + 1) * wide)
            gate_pre = product(wg, q, lo, hi)
            up_pre = product(wu, q, lo, hi)
            if k > 0:
                gate_pre = gate_pre + acc[0, :, cols]
                up_pre = up_pre + acc[1, :, cols]
            if k < n_k - 1:
                acc[0, :, cols] = gate_pre
                acc[1, :, cols] = up_pre
                if q == 0:
                    third(k + 1)
                continue
            y = (gate_pre * jax.nn.sigmoid(gate_pre) * up_pre).astype(BF16).astype(F32)
            g = [jnp.broadcast_to(gates[:, q * quad + i:q * quad + i + 1], (n_tok, 128)) for i in range(quad)]
            scale = []
            for lane0 in range(0, wide, 128):
                i = lane0 // ff
                edge = (i + 1) * ff - lane0
                scale.append(g[i] if edge >= 128 else jnp.where(lane < edge, g[i], g[i + 1]))
            act[:, cols] = (y * jnp.concatenate(scale, axis=-1)).astype(BF16)
    for p in range(n_pair):
        wcopy(2, p).wait()
    c0, c1, c2 = {}, {}, {}

    groups = []
    for j in range(n_cols):
        if starts[j] % 512 == 0:
            groups.append([])
        groups[-1].append(j)

    def down(i):
        lo, wide_n = starts[groups[i][0]], sum(widths[j] for j in groups[i])
        both = jnp.dot(act[...], wd[:, :, lo:lo + wide_n].reshape(n_exp * ff, wide_n), preferred_element_type=F32)
        for j in groups[i]:
            o32, c0_send, c0_recv = cbufs[j][0:3]
            o = both[:, starts[j] - lo:starts[j] - lo + widths[j]].reshape(n_x, 2, n_tp, rows, widths[j])
            o32[...] = o
            c0_send[...] = o.astype(BF16)
            c0[j] = send(c0_send.at[:, 1 - c], c0_recv, c0_ss.at[j], c0_rs.at[j], partner)

    def stage1(j):
        o32, _, c0_recv, c1_send, c1_own, c1_recv = cbufs[j][0:6]
        c0[j].wait_recv()
        total = o32[:, c] + c0_recv[...].astype(F32)
        c1_send[...] = total.astype(BF16)
        c1_own[...] = total
        c1[j] = [send(c1_send.at[x_dst(dx)], c1_recv.at[dx - 1], c1_ss.at[j, dx - 1], c1_rs.at[j, dx - 1], x_peer(dx)) for dx in range(1, n_x)]

    def stage2(j):
        c1_own, c1_recv, c2_buf = cbufs[j][4:7]
        total = c1_own[x]
        for dx in range(1, n_x):
            c1[j][dx - 1].wait_recv()
            total = total + c1_recv[dx - 1].astype(F32)
        c2_buf[t] = total.astype(BF16)
        c2[j] = [send(c2_buf.at[t], c2_buf.at[t], c2_ss.at[j, dt - 1], c2_rs.at[j, dt - 1], y_peer(dt)) for dt in range(1, n_tp)]

    outs = []

    def stage3(j):
        c2_buf = cbufs[j][6]
        if j == 0:
            for cp in x1_sends:
                cp.wait_recv()
        for cp in c2[j]:
            cp.wait_recv()
        cols = slice(starts[j], starts[j] + widths[j])
        total = c2_buf[0].astype(F32)
        for i in range(1, n_tp):
            total = total + c2_buf[i].astype(F32)
        outbuf[:, :, cols] = (x1_s[:, :, cols].astype(F32) + total).astype(BF16)
        where = (slice(None), slice(None), pl.ds(starts[j], widths[j]))
        cp = pltpu.make_async_copy(outbuf.at[where], out_hbm.at[where], sem_out.at[j])
        cp.start()
        outs.append(cp)

    plan = [(down, i, i) for i in range(len(groups))]
    for i, group in enumerate(groups):
        for n, j in enumerate(group):
            plan.append((stage1, j, i + 1.25 + 0.05 * n if i < len(groups) - 1 else i + 0.7 + 0.05 * n))
            plan.append((stage2, j, len(groups) - 0.4 + starts[j] / 400))
            plan.append((stage3, j, len(groups) + 2.0 + starts[j] / 400))
    for stage, j, _ in sorted(plan, key=lambda one: one[2]):
        stage(j)
    for cp in sent:
        cp.wait_send()
    for cp in outs:
        cp.wait()


def solution(mesh):
    n_ep = mesh.shape['ep']
    n_tp = mesh.shape['tp']
    n_x = n_ep // 2
    token_rows = P(('dp', 'ep'), None)
    token_vec = P(('dp', 'ep'))
    cache_spec = P(('dp', 'ep'), None, 'tp', None)
    expert_in = P('ep', None, 'tp')
    expert_down = P('ep', 'tp', None)
    hbm_spec = pl.BlockSpec(memory_space=pltpu.HBM)

    def device_step(hidden, seq_lens, rope_cos, rope_sin, ln1_scale, ln1_bias, w_qkv, b_qkv, w_out, b_out, k_cache, v_cache, ln2_scale, ln2_bias, w_router, expert_ids, w_gate, w_up, w_down):
        n_batch, d_model = hidden.shape
        _, s_max, n_kv, head = k_cache.shape
        n_q = w_qkv.shape[1] // head - 2
        rows = n_batch // n_tp
        n_qkv, group = 4, 8
        k3 = k_cache.reshape(n_batch, s_max, head)
        v3 = v_cache.reshape(n_batch, s_max, head)
        dma = pltpu.SemaphoreType.DMA
        ctx, k_out, v_out = pl.pallas_call(
            functools.partial(attention_kernel, n_qkv, group),
            out_shape=(jax.ShapeDtypeStruct((n_batch, n_q * head), BF16), jax.ShapeDtypeStruct(k3.shape, BF16), jax.ShapeDtypeStruct(v3.shape, BF16)),
            in_specs=[hbm_spec] * 10,
            out_specs=(hbm_spec,) * 3,
            scratch_shapes=[
                pltpu.SMEM(seq_lens.shape, jnp.int32),
                pltpu.VMEM(hidden.shape, BF16),
                pltpu.VMEM(rope_cos.shape, F32),
                pltpu.VMEM(rope_sin.shape, F32),
                pltpu.VMEM((d_model,), BF16),
                pltpu.VMEM((d_model,), BF16),
                pltpu.VMEM(b_qkv.shape, BF16),
                dma((7,)),
                pltpu.VMEM(w_qkv.shape, BF16),
                pltpu.VMEM(k3.shape, BF16),
                pltpu.VMEM(v3.shape, BF16),
                pltpu.VMEM((n_batch, n_q, head), F32),
                pltpu.VMEM((n_batch, n_q, head), F32),
                pltpu.VMEM((2, n_batch, head), F32),
                pltpu.VMEM((n_batch, n_q * head), BF16),
                dma((n_qkv,)), dma((n_batch // group,)), dma((n_batch // group,)), dma((n_batch // group,)), dma((n_batch // group,)),
            ],
            compiler_params=pltpu.CompilerParams(vmem_limit_bytes=63 * 1024 * 1024),
            name='attention',
        )(seq_lens, hidden, rope_cos, rope_sin, ln1_scale, ln1_bias, b_qkv, w_qkv, k3, v3)

        widths = (512, 512, 512, 256, 256)
        n_cols = len(widths)
        n_k, n_o = 2, 4
        quarter = d_model // (2 * n_k)
        wg = jnp.swapaxes(w_gate, 1, 2)
        wu = jnp.swapaxes(w_up, 1, 2)
        n_exp, ff, _ = wg.shape
        n_all = w_router.shape[1]
        n_tok = n_ep * n_batch
        ids_t = expert_ids.T
        V = pltpu.VMEM
        nx1, nt1 = n_x - 1, n_tp - 1
        assert n_tp == n_x
        out = pl.pallas_call(
            functools.partial(moe_kernel, n_tp, n_x, widths),
            out_shape=jax.ShapeDtypeStruct((n_tp, rows, d_model), BF16),
            in_specs=[hbm_spec] * 11,
            out_specs=hbm_spec,
            scratch_shapes=[
                V(ctx.shape, BF16), V((rows, d_model), BF16), V(ids_t.shape, jnp.int32),
                V((d_model,), BF16), V((d_model,), BF16), V((d_model,), BF16), V(w_out.shape, BF16), V(w_router.shape, BF16),
                V(wg.shape, BF16), V(wg.shape, BF16), V(wg.shape, BF16),
                V((n_tp, rows, n_all), F32),
                V((n_o, n_tp, rows, d_model // n_o), BF16),
                V((n_o, nt1, rows, d_model // n_o), BF16),
                V((n_tp, rows, d_model), BF16),
                V((n_k, n_x, 2, n_tp, rows, quarter), BF16),
                V((n_k, n_x, 2, n_tp, rows, quarter + n_all), BF16),
                V((n_tok, d_model), BF16),
                V((2, n_tok, n_exp * ff), F32),
                V((n_tok, n_exp * ff), BF16),
                V((n_tp, rows, d_model), BF16),
                [(V((n_x, 2, n_tp, rows, w), F32), V((n_x, 2, n_tp, rows, w), BF16), V((n_x, n_tp, rows, w), BF16),
                  V((n_x, n_tp, rows, w), BF16), V((n_x, n_tp, rows, w), F32), V((nx1, n_tp, rows, w), BF16), V((n_tp, n_tp, rows, w), BF16)) for w in widths],
                dma((7,)), dma((n_o,)), dma((3, n_exp // 2)),
                dma((n_o, nt1)), dma((n_o, nt1)),
                dma((n_k, 2, nx1)), dma((n_k, 2, nx1)), dma((n_k, 2, nx1)), dma((n_k, 2, nx1)), dma((n_k, 2, n_x)), dma((n_k, 2, n_x)),
                dma((nt1,)), dma((nt1,)),
                dma((n_cols,)), dma((n_cols,)), dma((n_cols, nx1)), dma((n_cols, nx1)), dma((n_cols, nt1)), dma((n_cols, nt1)),
                dma((n_cols,)),
            ],
            compiler_params=pltpu.CompilerParams(vmem_limit_bytes=63 * 1024 * 1024, collective_id=0, has_side_effects=True),
            name='moe',
        )(ctx, hidden.reshape(n_tp, rows, d_model), ids_t, b_out, ln2_scale, ln2_bias, w_out, w_router, wg, wu, w_down)
        return out.reshape(n_batch, d_model), k_out.reshape(k_cache.shape), v_out.reshape(v_cache.shape)

    in_specs = (token_rows, token_vec, token_rows, token_rows, P(), P(), P(None, 'tp'), P('tp'), P('tp', None), P(), cache_spec, cache_spec, P(), P(), P(), token_rows, expert_in, expert_in, expert_down)
    return jax.shard_map(device_step, mesh=mesh, in_specs=in_specs, out_specs=(token_rows, cache_spec, cache_spec), check_vma=False)
```

time: 58.6 us -> 54.8 us (0.935)
  the two profiles are of different devices: /device:TPU:96 before, /device:TPU:97 now
where the time goes in v3:
time: 54.8 us; the launch traced here: 54.3 us
  Pallas kernels  52.1 us (95%)
  local copies, waits for them, and re-layouts  1.57 us (3%)
  between operations  0.65 us (1%)
    pallas_call x1, Pallas kernels, device_step(): pl.pallas_call(functools.partial(moe_kernel, n_tp, n_x, widths), out_shap...  45.6 us
    pallas_call x1, Pallas kernels, device_step(): pl.pallas_call(functools.partial(attention_kernel, n_qkv, group), out_sha...  6.47 us
    unnamed x1, local copies, waits for them, and re-layouts  1.57 us

profile of v3, /device:TPU:97, one launch (start us, length us, event | category | flops | bytes accessed | tf_op | source)
XLA Modules:
  0.0 54.3 jit_solution(2015321772012174590)
XLA Ops:
  0.6 6.5 %attention.1 = (bf16[32,1024]{1,0:T(8,128)(2,1)}, bf16[32,256,128]{2,1,0:T(8,128)(2,1)}, bf16[32,256,128]{2,1,0:T(8,128)(2,1)}) custom-call(s32[32]{0:T(128)} %seq_hbm.1, bf16[32,2048]{1,0:T(8,128)(2,1)} %hid_hbm.1, f32[32,64]{1,0:T(8,128)} %cos_hbm.1, f32[32,64]{1,0:T(8,128)} %sin_hbm.1, bf16[2048]{0:T(1024)(128)(2,1)} %lns_hbm.2, bf16[2048]{0:T(1024)(128)(2,1)} %lnb_hbm.2, ...), custom_call_target="tpu_custom_call" | custom-call | tf_op jit(solution)/shard_map/attention/pallas_call | solution.py:388
  7.1 45.6 %moe.1 = bf16[4,8,2048]{2,1,0:T(8,128)(2,1)} custom-call(bf16[32,1024]{1,0:T(8,128)(2,1)} %get-tuple-element.6.ctx_hbm, bf16[4,8,2048]{2,1,0:T(8,128)(2,1)} %bitcast.18, s32[8,32]{1,0:T(8,128)} %bitcast.19, bf16[2048]{0:T(1024)(128)(2,1)} %bout_hbm.1, bf16[2048]{0:T(1024)(128)(2,1)} %lns_hbm.3, bf16[2048]{0:T(1024)(128)(2,1)} %lnb_hbm.3, ...), custom_call_target="tpu_custom_call" | custom-call | tf_op jit(solution)/shard_map/moe/pallas_call | solution.py:428
  52.7 1.6 %copy.25 = bf16[32,2048]{1,0:T(8,128)(2,1)} copy(bf16[32,2048]{1,0:T(8,128)(2,1)} %bitcast.17) | data formatting | bytes 262144
